TPU v7x, 256 devices: a whole 4x4x8 slice. The times are simulated.
256 devices in a mesh: band: 4 (over x), pulse: 16 (over y, z_lo, core), range: 4 (over z_hi).
Axes of the slice: x: 4, y: 4, z: 8 (z_hi: 4, z_lo: 2; z = z_hi * 2 + z_lo), core: 2. Of those that a mesh axis runs over, the one named last changes fastest.
Arguments:
- echoes: bfloat16 [4, 2, 8192, 4096], P('band', None, 'pulse', 'range'), may hold values from -6 to 6
- range_phase: float32 [4, 4096], P('band'), may hold values from -3.140625 to 3.140625
- pulse_shift: int32 [4, 8192], P('band', ('pulse', 'range')), may hold values from -64 to 64
- bin_offset: int32 [4], replicated, may hold values from 0 to 1024, as said below
- doppler_phase: float32 [8192], replicated, may hold values from -3.140625 to 3.140625
Outputs:
- focused: bfloat16 [12288, 2, 8192], P(('band', 'pulse', 'range'))
Inputs may be any that keep to these rules, and one draw needn't show every extreme that they name: Band b's spectrum begins at combined bin b * 3072 - 2 * 512 + bin_offset[b]. In every draw some band other than the last has offset 2 * 512 and the band after it has offset 0.
All inputs are finite; a program needn't handle non-finite values.
Results may differ from a plain program's by a relative error of at most 0.0054.
Values may be sent and summed in bfloat16 or wider, within the bound.
No kernel may reach another device: no remote copies, remote signals or barrier semaphores. Data moves between devices by JAX's collectives and lax.ppermute only.
A program may use at most 64 MiB of HBM per device.

v0:
```python
import functools
import math

import jax
import jax.numpy as jnp
import ml_dtypes
import numpy as np
from jax import lax
from jax.experimental import pallas as pl
from jax.experimental.pallas import tpu as pltpu
from jax.sharding import PartitionSpec as P

MARGIN = 512
LANES = 128
F32 = jnp.float32
BF16 = jnp.bfloat16


def split_const(table):
    high = table.astype(ml_dtypes.bfloat16)
    low = (table - high.astype(np.float64)).astype(ml_dtypes.bfloat16)
    return high, low


def unit_roots(rows, cols, modulus, sign):
    product = np.outer(np.arange(rows), np.arange(cols)) % modulus
    angle = sign * 2.0 * np.pi * product / modulus
    return np.cos(angle), np.sin(angle)


def split_value(value):
    high = value.astype(BF16)
    low = (value - high.astype(F32)).astype(BF16)
    return high, low


def dot_f32(lhs, rhs, contract):
    return lax.dot_general(lhs, rhs, (contract, ((), ())), preferred_element_type=F32)


def dot_three(lhs, rhs, contract):
    return (
        dot_f32(lhs[0], rhs[0], contract)
        + dot_f32(lhs[0], rhs[1], contract)
        + dot_f32(lhs[1], rhs[0], contract)
    )


def complex_mul(a, b):
    return a[0] * b[0] - a[1] * b[1], a[0] * b[1] + a[1] * b[0]


def by_constant(a, angle):
    cos = math.cos(angle)
    sin = math.sin(angle)
    quarter = angle / (math.pi / 2)
    if abs(quarter - round(quarter)) < 1e-9:
        turn = int(round(quarter)) % 4
        if turn == 0:
            return a
        if turn == 1:
            return -a[1], a[0]
        if turn == 2:
            return -a[0], -a[1]
        return a[1], -a[0]
    if abs(abs(cos) - abs(sin)) < 1e-9:
        half = math.sqrt(0.5)
        plus = (a[0] + a[1]) * half
        minus = (a[0] - a[1]) * half
        if cos > 0 and sin > 0:
            return minus, plus
        if cos < 0 and sin > 0:
            return -plus, minus
        if cos < 0 and sin < 0:
            return -minus, -plus
        return plus, -minus
    return a[0] * cos - a[1] * sin, a[0] * sin + a[1] * cos


def small_dft(values, sign):
    count = len(values)
    if count == 1:
        return values
    even = small_dft(values[0::2], sign)
    odd = small_dft(values[1::2], sign)
    first = []
    second = []
    for i in range(count // 2):
        turned = by_constant(odd[i], sign * 2.0 * math.pi * i / count)
        first.append((even[i][0] + turned[0], even[i][1] + turned[1]))
        second.append((even[i][0] - turned[0], even[i][1] - turned[1]))
    return first + second


def range_kernel(outer, sub, rows, shift_ref, echo_ref, twist_ref, cos_ref, sin_ref,
                 high_ref, low_ref, out_ref, stage_ref, mid_ref):
    step = pl.program_id(0)
    sources = echo_ref.shape[0]
    inner = outer // sources
    group = 16

    @pl.when(step == 0)
    def _():
        def block(t, carry):
            at = pl.multiple_of(t * group, group)
            for n in range(inner):
                lanes = slice(n * LANES, (n + 1) * LANES)
                values = []
                for z in range(sources):
                    values.append((
                        echo_ref[z, 0, pl.ds(at, group), lanes].astype(F32),
                        echo_ref[z, 1, pl.ds(at, group), lanes].astype(F32),
                    ))
                for q, value in enumerate(small_dft(values, -1.0)):
                    value = by_constant(value, -2.0 * math.pi * n * q / outer)
                    mid_ref[q, n, 0] = value[0]
                    mid_ref[q, n, 1] = value[1]
            for q in range(sources):
                values = [(mid_ref[q, n, 0], mid_ref[q, n, 1]) for n in range(inner)]
                for m, value in enumerate(small_dft(values, -1.0)):
                    stage_ref[q + sources * m, 0, pl.ds(at, group), :] = value[0]
                    stage_ref[q + sources * m, 1, pl.ds(at, group), :] = value[1]
            return carry

        lax.fori_loop(0, rows // group, block, 0)

    shift = shift_ref[0]
    per_step = cos_ref.shape[0]
    for i in range(per_step):
        real_rows = []
        imag_rows = []
        for h in range(sub):
            bin_low = (step * per_step + i) * sub + h
            source = lax.rem(bin_low - shift + 2 * outer, outer)
            twist = (twist_ref[0, pl.ds(bin_low, 1), :], twist_ref[1, pl.ds(bin_low, 1), :])
            value = complex_mul((stage_ref[source, 0], stage_ref[source, 1]), twist)
            real_rows.append(value[0])
            imag_rows.append(value[1])
        real = jnp.concatenate(real_rows, axis=0) if sub > 1 else real_rows[0]
        imag = jnp.concatenate(imag_rows, axis=0) if sub > 1 else imag_rows[0]
        data = split_value(jnp.concatenate((real, imag), axis=1))
        product = dot_three((high_ref[...], low_ref[...]), data, ((1,), (1,)))
        half = product.shape[0] // 2
        value = product[:half] * cos_ref[i] + product[half:] * sin_ref[i]
        out_ref[i] = value.astype(BF16)


def range_tables():
    cos, sin = unit_roots(LANES, LANES, LANES, -1.0)
    plain = np.zeros((LANES, 2, 2, LANES))
    turned = np.zeros((LANES, 2, 2, LANES))
    plain[:, 0, 0], plain[:, 0, 1] = cos, -sin
    plain[:, 1, 0], plain[:, 1, 1] = sin, cos
    turned[:, 0] = -plain[:, 1]
    turned[:, 1] = plain[:, 0]
    return split_const(np.concatenate((plain, turned)).reshape(4 * LANES, 2 * LANES))


def range_stage(received, twist, cos, sin, shift, outer, sub):
    rows = received.shape[2]
    steps = cos.shape[0]
    per_step = 2
    high, low = range_tables()
    kernel = functools.partial(range_kernel, outer, sub, rows)
    whole = lambda shape: pl.BlockSpec(shape, lambda i: (0,) * len(shape))
    return pl.pallas_call(
        kernel,
        grid=(steps // per_step,),
        in_specs=[
            pl.BlockSpec(memory_space=pltpu.SMEM),
            whole(received.shape),
            whole(twist.shape),
            pl.BlockSpec((per_step, 2 * LANES, LANES), lambda i: (i, 0, 0)),
            pl.BlockSpec((per_step, 2 * LANES, LANES), lambda i: (i, 0, 0)),
            whole(high.shape),
            whole(low.shape),
        ],
        out_specs=pl.BlockSpec((per_step, 2 * LANES, LANES), lambda i: (i, 0, 0)),
        out_shape=jax.ShapeDtypeStruct((steps, 2 * LANES, LANES), BF16),
        scratch_shapes=[
            pltpu.VMEM((outer, 2, rows, LANES), F32),
            pltpu.VMEM((received.shape[0], outer // received.shape[0], 2, 16, LANES), F32),
        ],
        compiler_params=pltpu.CompilerParams(
            dimension_semantics=("arbitrary",), vmem_limit_bytes=48 * 1024 * 1024),
        name="range_stage",
    )(shift, received, twist, cos, sin, jnp.asarray(high), jnp.asarray(low))


def azimuth_kernel(outer, first_ref, fore_ref, twist_ref, filter_ref, back_ref, last_ref,
                   data_ref, out_ref):
    count = data_ref.shape[0]
    twist = (twist_ref[0], twist_ref[1])
    twist_back = (twist_ref[0], -twist_ref[1])
    turn = (filter_ref[0], filter_ref[1])
    left = ((1,), (0,))
    rows = []
    for c in range(count):
        spread = dot_f32(first_ref[0], data_ref[c], left) + dot_f32(first_ref[1], data_ref[c], left)
        value = complex_mul((spread[:outer], spread[outer:]), twist)
        rows.append(jnp.concatenate(value, axis=1))
    stacked = split_value(jnp.concatenate(rows, axis=0))
    doppler = dot_three(stacked, (fore_ref[0], fore_ref[1]), left)
    rows = []
    for c in range(count):
        part = doppler[c * outer:(c + 1) * outer]
        rows.append(jnp.concatenate(complex_mul((part[:, :LANES], part[:, LANES:]), turn), axis=1))
    stacked = split_value(jnp.concatenate(rows, axis=0))
    image = dot_three(stacked, (back_ref[0], back_ref[1]), left)
    for c in range(count):
        part = image[c * outer:(c + 1) * outer]
        value = complex_mul((part[:, :LANES], part[:, LANES:]), twist_back)
        value = split_value(jnp.concatenate(value, axis=0))
        out_ref[c] = dot_three((last_ref[0], last_ref[1]), value, left).astype(BF16)


def azimuth_tables(outer):
    cos, sin = unit_roots(outer, outer, outer, -1.0)
    first = np.zeros((2, outer, outer, 2))
    first[0, :, :, 0], first[0, :, :, 1] = cos, -sin
    first[1, :, :, 0], first[1, :, :, 1] = sin, cos
    last = np.zeros((outer, 2, 2, outer))
    last[:, 0, 0], last[:, 0, 1] = cos, sin
    last[:, 1, 0], last[:, 1, 1] = -sin, cos
    cos, sin = unit_roots(LANES, LANES, LANES, -1.0)
    fore = np.zeros((2, LANES, 2, LANES))
    fore[0, :, 0], fore[0, :, 1] = cos, sin
    fore[1, :, 0], fore[1, :, 1] = -sin, cos
    back = np.zeros((2, LANES, 2, LANES))
    back[0, :, 0], back[0, :, 1] = cos, -sin
    back[1, :, 0], back[1, :, 1] = sin, cos
    pair = lambda table, shape: np.stack(split_const(table.reshape(shape)))
    twist = np.stack(unit_roots(outer, LANES, outer * LANES, -1.0)).astype(np.float32)
    square = (2 * LANES, 2 * LANES)
    side = (2 * outer, 2 * outer)
    return pair(first, side), pair(fore, square), twist, pair(back, square), pair(last, side)


def azimuth_stage(data, turn, outer):
    count = data.shape[0]
    block = 8
    first, fore, twist, back, last = azimuth_tables(outer)
    whole = lambda shape: pl.BlockSpec(shape, lambda i: (0,) * len(shape))
    tile = pl.BlockSpec((block,) + data.shape[1:], lambda i: (i, 0, 0))
    constants = (first, fore, twist)
    return pl.pallas_call(
        functools.partial(azimuth_kernel, outer),
        grid=(count // block,),
        in_specs=[whole(first.shape), whole(fore.shape), whole(twist.shape), whole(turn.shape),
                  whole(back.shape), whole(last.shape), tile],
        out_specs=tile,
        out_shape=jax.ShapeDtypeStruct(data.shape, BF16),
        compiler_params=pltpu.CompilerParams(
            dimension_semantics=("arbitrary",), vmem_limit_bytes=48 * 1024 * 1024),
        name="azimuth_stage",
    )(jnp.asarray(first), jnp.asarray(fore), jnp.asarray(twist), turn, jnp.asarray(back),
      jnp.asarray(last), data)


def shifted(block, distance):
    devices = range(lax.axis_size("band"))
    route = [(i - distance, i) for i in devices if i - distance in devices]
    return lax.ppermute(block, "band", route)


def body(echoes, range_phase, pulse_shift, bin_offset, doppler_phase):
    range_count = lax.axis_size("range")
    group_size = lax.axis_size("pulse") * range_count
    cells_local = echoes.shape[3]
    cell_count = cells_local * range_count
    n_local = echoes.shape[2] // range_count
    spill_len = 2 * MARGIN
    owned_bins = cell_count - spill_len
    bins_local = owned_bins // group_size
    outer = cell_count // LANES
    sub = 1

    band = lax.axis_index("band")
    bands = bin_offset.shape[0]
    order = jnp.arange(bands, dtype=jnp.int32)
    offset_of = lambda index: jnp.sum(jnp.where(order == index, bin_offset, 0))
    offset = offset_of(band)
    below = offset_of(band - 1)
    above = offset_of(band + 1)
    shift = offset - spill_len

    rows_in = echoes[0].reshape(2, range_count, n_local, cells_local)
    rows_in = jnp.transpose(rows_in, (1, 0, 2, 3))
    received = lax.all_to_all(rows_in, "range", split_axis=0, concat_axis=0, tiled=True)

    low = jnp.arange(outer, dtype=jnp.int32)
    lane = jnp.arange(LANES, dtype=jnp.int32)
    angle = jnp.mod((low[:, None] - shift) * lane[None, :], cell_count).astype(F32) * (
        -2.0 * math.pi / cell_count)
    twist = jnp.stack((jnp.cos(angle), jnp.sin(angle)))
    phase = jnp.concatenate((range_phase[0], range_phase[0]))
    phase = lax.dynamic_slice_in_dim(phase, spill_len - offset, cell_count, 0)
    phase = jnp.transpose(phase.reshape(LANES, outer))
    index = jnp.mod(low[:, None] + outer * lane[None, :] - shift, cell_count)
    ramp = jnp.mod(index[:, :, None] * pulse_shift[0][None, None, :], cell_count).astype(F32) * (
        -2.0 * math.pi / cell_count)
    theta = phase[:, :, None] + ramp
    double = lambda value: jnp.broadcast_to(
        value[:, :, None, :], (outer, LANES, 2, LANES)).reshape(outer, 2 * LANES, LANES)
    scale = 1.0 / math.sqrt(cell_count)
    cos = double(jnp.cos(theta) * scale)
    sin = double(jnp.sin(theta) * scale)

    spectrum = range_stage(received, twist, cos, sin, shift.reshape(1), outer, sub)
    spectrum = jnp.transpose(spectrum.reshape(outer, LANES, 2, LANES), (1, 0, 2, 3))
    spectrum = spectrum.reshape(cell_count, 2, LANES)
    spill = spectrum[owned_bins:]
    from_below = shifted(spill, 1)
    from_above = shifted(spill, -1)
    row = jnp.arange(spill_len, dtype=jnp.int32)[:, None, None]
    add_low = jnp.where(row < below, from_below.astype(F32), 0.0)
    add_high = jnp.where(row >= above, from_above.astype(F32), 0.0)
    first = spectrum[:spill_len].astype(F32) + add_low
    middle = spectrum[spill_len:owned_bins - spill_len]
    final = spectrum[owned_bins - spill_len:owned_bins].astype(F32) + add_high
    stitched = jnp.concatenate((first.astype(BF16), middle, final.astype(BF16)))
    blocks = stitched.reshape(group_size, bins_local, 2, LANES)
    samples = lax.all_to_all(blocks, ("pulse", "range"), split_axis=0, concat_axis=0, tiled=True)

    samples = jnp.transpose(samples, (1, 0, 2, 3)).reshape(bins_local, 2 * group_size, LANES)
    doppler = jnp.transpose(doppler_phase.reshape(LANES, group_size))
    factor = 1.0 / doppler_phase.shape[0]
    turn = jnp.stack((jnp.cos(doppler) * factor, jnp.sin(doppler) * factor))
    image = azimuth_stage(samples, turn, group_size)
    image = jnp.transpose(image.reshape(bins_local, group_size, 2, LANES), (0, 2, 1, 3))
    return image.reshape(bins_local, 2, group_size * LANES)


def solution(mesh):
    in_specs = (
        P("band", None, "pulse", "range"),
        P("band", None),
        P("band", ("pulse", "range")),
        P(),
        P(),
    )
    out_specs = P(("band", "pulse", "range"), None, None)
    return jax.shard_map(body, mesh=mesh, in_specs=in_specs, out_specs=out_specs, check_vma=False)
```

profile of v0, /device:TPU:2, one launch (start us, length us, event | category | flops | bytes accessed | tf_op | source)
XLA Modules:
  0.0 164.8 jit_solution(3830488142496182380)
XLA Ops:
  0.0 3.1 %copy.32 = bf16[2,4,128,1024]{3,2,0,1:T(8,128)(2,1)} copy(bf16[2,4,128,1024]{3,2,1,0:T(8,128)(2,1)} %bitcast.44) | data formatting | bytes 4194304 | tf_op jit(solution)/shard_map/reshape;squeeze | solution.py:287
  3.1 8.6 %all-to-all-start = ((bf16[4,2,128,1024]{3,2,1,0:T(8,128)(2,1)}), bf16[4,2,128,1024]{3,2,1,0:T(8,128)(2,1)S(1)}, u32[]{:S(2)}, u32[]{:S(2)}) async-start(bf16[4,2,128,1024]{3,2,1,0:T(8,128)(2,1)} %bitcast.40), calls=%async_computation | async-start | bytes 4194304 | tf_op jit(solution)/shard_map/all_to_all | solution.py:289
  11.7 0.7 fusion.17
  13.5 0.1 fusion.10
  13.6 0.1 reshape.214
  13.7 0.1 copy.24
  14.4 0.2 fusion.15
  14.6 13.1 %sine_multiply_fusion = (f32[32,128,128]{2,1,0:T(8,128)}, f32[32,128,128]{2,1,0:T(8,128)}) fusion(s32[128]{0:T(128)S(1)} %bitcast.52, s32[32,128]{1,0:T(8,128)S(1)} %add_select_fusion.1, f32[32,128]{1,0:T(8,128)S(1)} %copy.24), kind=kLoop, calls=%fused_computation.11 | loop fusion | flops 8912896 | bytes 4227584 | tf_op jit(solution)/shard_map/mul | solution.py:307
  27.7 34.8 %all-to-all-done.echo_ref = bf16[4,2,128,1024]{3,2,1,0:T(8,128)(2,1)S(1)} async-done(((bf16[4,2,128,1024]{3,2,1,0:T(8,128)(2,1)}), bf16[4,2,128,1024]{3,2,1,0:T(8,128)(2,1)S(1)}, u32[]{:S(2)}, u32[]{:S(2)}) %all-to-all-start) | async-done | bytes 2097184 | tf_op jit(solution)/shard_map/all_to_all | solution.py:289
  62.5 5.2 %broadcast_in_dim.44 = f32[32,128,2,128]{3,2,1,0:T(2,128)} broadcast(f32[32,128,128]{2,1,0:T(8,128)} %get-tuple-element.13), dimensions={0,1,3} | broadcast | bytes 6291456 | tf_op jit(solution)/shard_map/broadcast_in_dim | solution.py:303
  67.7 3.4 %broadcast_in_dim.45 = f32[32,128,2,128]{3,2,1,0:T(2,128)} broadcast(f32[32,128,128]{2,1,0:T(8,128)S(1)} %copy-done.7), dimensions={0,1,3} | broadcast | bytes 6291456 | tf_op jit(solution)/shard_map/broadcast_in_dim | solution.py:303
  71.1 15.4 %range_stage.1 = bf16[32,256,128]{2,1,0:T(8,128)(2,1)S(1)} custom-call(s32[1]{0:T(128)} %bitcast.4.shift_ref, bf16[4,2,128,1024]{3,2,1,0:T(8,128)(2,1)S(1)} %all-to-all-done.echo_ref, f32[2,32,128]{2,1,0:T(8,128)S(1)} %pad_maximum_fusion.2.twist_ref, f32[32,256,128]{2,1,0:T(8,128)} %bitcast.38, f32[32,256,128]{2,1,0:T(8,128)} %bitcast.39, ...), custom_call_target="tpu_custom_call" | custom-call | tf_op jit(solution)/shard_map/range_stage/pallas_call | solution.py:166
  86.5 1.4 copy.31
  87.9 0.4 fusion.19
  88.3 3.4 %collective-permute-start = (bf16[1024,2,128]{2,0,1:T(8,128)(2,1)S(1)}, bf16[1024,2,128]{2,0,1:T(8,128)(2,1)S(1)}, u32[]{:S(2)}, u32[]{:S(2)}) collective-permute-start(bf16[1024,2,128]{2,0,1:T(8,128)(2,1)S(1)} %bitcast.46), channel_id=1, source_target_pairs={{0,64},{64,128},{128,192},{1,65},{65,129},{129,193},{2,66},{66,130... | collective-permute-start | bytes 1572872 | tf_op jit(solution)/shard_map/ppermute | solution.py:263
  91.7 2.5 %collective-permute-start.1 = (bf16[1024,2,128]{2,0,1:T(8,128)(2,1)S(1)}, bf16[1024,2,128]{2,0,1:T(8,128)(2,1)S(1)}, u32[]{:S(2)}, u32[]{:S(2)}) collective-permute-start(bf16[1024,2,128]{2,0,1:T(8,128)(2,1)S(1)} %bitcast.47), channel_id=1, source_target_pairs={{64,0},{128,64},{192,128},{65,1},{129,65},{193,129},{66,2},{130,66... | collective-permute-start | bytes 1572872 | tf_op jit(solution)/shard_map/ppermute | solution.py:263
  94.2 1.3 iota_compare_fusion
  95.4 3.9 %collective-permute-done = bf16[1024,2,128]{2,0,1:T(8,128)(2,1)S(1)} collective-permute-done((bf16[1024,2,128]{2,0,1:T(8,128)(2,1)S(1)}, bf16[1024,2,128]{2,0,1:T(8,128)(2,1)S(1)}, u32[]{:S(2)}, u32[]{:S(2)}) %collective-permute-start) | collective-permute-done | bytes 524320 | tf_op jit(solution)/shard_map/ppermute | solution.py:263
  99.3 0.3 fusion.5
  99.7 3.1 %collective-permute-done.1 = bf16[1024,2,128]{2,0,1:T(8,128)(2,1)S(1)} collective-permute-done((bf16[1024,2,128]{2,0,1:T(8,128)(2,1)S(1)}, bf16[1024,2,128]{2,0,1:T(8,128)(2,1)S(1)}, u32[]{:S(2)}, u32[]{:S(2)}) %collective-permute-start.1) | collective-permute-done | bytes 524320 | tf_op jit(solution)/shard_map/ppermute | solution.py:263
  102.8 0.3 fusion.4
  103.1 0.1 pad_maximum_fusion
  103.2 1.3 copy.26
  104.5 9.3 %all-to-all-start.1 = ((bf16[64,48,2,128]{3,1,2,0:T(8,128)(2,1)}), bf16[64,48,2,128]{3,1,2,0:T(8,128)(2,1)S(1)}, u32[]{:S(2)}, u32[]{:S(2)}) async-start(bf16[64,48,2,128]{3,1,2,0:T(8,128)(2,1)} %copy.26), calls=%async_computation.1 | async-start | bytes 3145728 | tf_op jit(solution)/shard_map/all_to_all | solution.py:323
  113.9 0.1 cosine_multiply_fusion.1
  114.0 0.1 mul.120
  114.1 0.1 copy.21
  114.1 0.1 mul.123
  114.2 0.1 copy.22
  114.3 39.8 %all-to-all-done.1 = bf16[64,48,2,128]{3,1,2,0:T(8,128)(2,1)S(1)} async-done(((bf16[64,48,2,128]{3,1,2,0:T(8,128)(2,1)}), bf16[64,48,2,128]{3,1,2,0:T(8,128)(2,1)S(1)}, u32[]{:S(2)}, u32[]{:S(2)}) %all-to-all-start.1) | async-done | bytes 1572896 | tf_op jit(solution)/shard_map/all_to_all | solution.py:323
  154.1 1.7 %copy.27 = bf16[48,64,2,128]{3,2,1,0:T(2,128)(2,1)S(1)} copy(bf16[48,64,2,128]{3,0,2,1:T(8,128)(2,1)S(1)} %bitcast.42) | data formatting | bytes 3145728 | tf_op jit(solution)/shard_map/transpose | solution.py:325
  155.9 9.0 %azimuth_stage.1 = bf16[48,128,128]{2,1,0:T(8,128)(2,1)} custom-call(bf16[2,128,128]{2,1,0:T(8,128)(2,1)S(1)} %copy-done.4, bf16[2,256,256]{2,1,0:T(8,128)(2,1)S(1)} %copy-done.2, f32[2,64,128]{2,1,0:T(8,128)S(1)} %copy-done.5, f32[2,64,128]{2,1,0:T(8,128)S(1)} %pad_maximum_fusion.1.filter_ref, bf16[2,256,256]{2,1,0:T(8,128)(2,1)S(1)} %copy-done.3, ...), custom_call_target="tpu_custom_call" | custom-call | tf_op jit(solution)/shard_map/azimuth_stage/pallas_call | solution.py:246
  (29 shorter events, 0.1 us)
Async XLA Ops:
  3.1 8.6 %copy-start.11 = (s32[4]{0:T(128)S(1)}, s32[4]{0:T(128)}, u32[]{:S(2)}) copy-start(s32[4]{0:T(128)} %param.15) | copy-start | bytes 52
  3.1 10.4 %copy-start.9 = (f32[1,4096]{1,0:T(1,128)S(1)}, f32[1,4096]{1,0:T(1,128)}, u32[]{:S(2)}) copy-start(f32[1,4096]{1,0:T(1,128)} %param.13) | copy-start | bytes 49156
  3.1 11.4 %copy-start.10 = (s32[1,128]{1,0:T(1,128)S(1)}, s32[1,128]{1,0:T(1,128)}, u32[]{:S(2)}) copy-start(s32[1,128]{1,0:T(1,128)} %param.14) | copy-start | bytes 1540
  3.1 59.4 %all-to-all-start = ((bf16[4,2,128,1024]{3,2,1,0:T(8,128)(2,1)}), bf16[4,2,128,1024]{3,2,1,0:T(8,128)(2,1)S(1)}, u32[]{:S(2)}, u32[]{:S(2)}) async-start(bf16[4,2,128,1024]{3,2,1,0:T(8,128)(2,1)} %bitcast.40), calls=%async_computation | async-start | bytes 4194304 | tf_op jit(solution)/shard_map/all_to_all | solution.py:289
  62.5 5.2 %copy-start.7 = (f32[32,128,128]{2,1,0:T(8,128)S(1)}, f32[32,128,128]{2,1,0:T(8,128)}, u32[]{:S(2)}) copy-start(f32[32,128,128]{2,1,0:T(8,128)} %get-tuple-element.12) | copy-start | bytes 6291460
  67.7 3.5 %copy-start = (bf16[512,256]{1,0:T(8,128)(2,1)S(1)}, bf16[512,256]{1,0:T(8,128)(2,1)}, u32[]{:S(2)}) copy-start(bf16[512,256]{1,0:T(8,128)(2,1)} %constant.71.clone.high_ref) | copy-start | bytes 786436
  67.7 3.5 %copy-start.1 = (bf16[512,256]{1,0:T(8,128)(2,1)S(1)}, bf16[512,256]{1,0:T(8,128)(2,1)}, u32[]{:S(2)}) copy-start(bf16[512,256]{1,0:T(8,128)(2,1)} %constant.72.clone.low_ref) | copy-start | bytes 786436
  88.3 11.1 %collective-permute-start = (bf16[1024,2,128]{2,0,1:T(8,128)(2,1)S(1)}, bf16[1024,2,128]{2,0,1:T(8,128)(2,1)S(1)}, u32[]{:S(2)}, u32[]{:S(2)}) collective-permute-start(bf16[1024,2,128]{2,0,1:T(8,128)(2,1)S(1)} %bitcast.46), channel_id=1, source_target_pairs={{0,64},{64,128},{128,192},{1,65},{65,129},{129,193},{2,66},{66,130... | collective-permute-start | bytes 1572872 | tf_op jit(solution)/shard_map/ppermute | solution.py:263
  91.7 11.1 %collective-permute-start.1 = (bf16[1024,2,128]{2,0,1:T(8,128)(2,1)S(1)}, bf16[1024,2,128]{2,0,1:T(8,128)(2,1)S(1)}, u32[]{:S(2)}, u32[]{:S(2)}) collective-permute-start(bf16[1024,2,128]{2,0,1:T(8,128)(2,1)S(1)} %bitcast.47), channel_id=1, source_target_pairs={{64,0},{128,64},{192,128},{65,1},{129,65},{193,129},{66,2},{130,66... | collective-permute-start | bytes 1572872 | tf_op jit(solution)/shard_map/ppermute | solution.py:263
  104.5 9.3 %copy-start.8 = (f32[8192]{0:T(1024)S(1)}, f32[8192]{0:T(1024)}, u32[]{:S(2)}) copy-start(f32[8192]{0:T(1024)} %param.16) | copy-start | bytes 98308
  104.5 49.7 %all-to-all-start.1 = ((bf16[64,48,2,128]{3,1,2,0:T(8,128)(2,1)}), bf16[64,48,2,128]{3,1,2,0:T(8,128)(2,1)S(1)}, u32[]{:S(2)}, u32[]{:S(2)}) async-start(bf16[64,48,2,128]{3,1,2,0:T(8,128)(2,1)} %copy.26), calls=%async_computation.1 | async-start | bytes 3145728 | tf_op jit(solution)/shard_map/all_to_all | solution.py:323
  113.8 42.0 %copy-start.2 = (bf16[2,256,256]{2,1,0:T(8,128)(2,1)S(1)}, bf16[2,256,256]{2,1,0:T(8,128)(2,1)}, u32[]{:S(2)}) copy-start(bf16[2,256,256]{2,1,0:T(8,128)(2,1)} %constant.74.clone.fore_ref) | copy-start | bytes 786436
  113.8 42.0 %copy-start.3 = (bf16[2,256,256]{2,1,0:T(8,128)(2,1)S(1)}, bf16[2,256,256]{2,1,0:T(8,128)(2,1)}, u32[]{:S(2)}) copy-start(bf16[2,256,256]{2,1,0:T(8,128)(2,1)} %constant.76.clone.back_ref) | copy-start | bytes 786436
  113.8 42.0 %copy-start.4 = (bf16[2,128,128]{2,1,0:T(8,128)(2,1)S(1)}, bf16[2,128,128]{2,1,0:T(8,128)(2,1)}, u32[]{:S(2)}) copy-start(bf16[2,128,128]{2,1,0:T(8,128)(2,1)} %constant.73.clone.first_ref) | copy-start | bytes 196612
  113.8 42.0 %copy-start.5 = (f32[2,64,128]{2,1,0:T(8,128)S(1)}, f32[2,64,128]{2,1,0:T(8,128)}, u32[]{:S(2)}) copy-start(f32[2,64,128]{2,1,0:T(8,128)} %constant.75.clone.twist_ref) | copy-start | bytes 196612
  113.8 42.0 %copy-start.6 = (bf16[2,128,128]{2,1,0:T(8,128)(2,1)S(1)}, bf16[2,128,128]{2,1,0:T(8,128)(2,1)}, u32[]{:S(2)}) copy-start(bf16[2,128,128]{2,1,0:T(8,128)(2,1)} %constant.77.clone.last_ref) | copy-start | bytes 196612
where the time goes:
time: 166 us; the launch traced here: 165 us
  waiting for transfers between devices  81.6 us (49%)
  Pallas kernels  24.3 us (15%)
  starting transfers between devices  23.8 us (14%)
  local copies, waits for them, and re-layouts  16.9 us (10%)
  other arithmetic  16.3 us (10%)
  between operations  1.96 us (1%)
    all_to_all x1, waiting for transfers between devices, body(): lax.all_to_all(blocks, ('pulse', 'range'), split_axis=0, concat_axis=0, t...  39.8 us
    all_to_all x1, waiting for transfers between devices, body(): lax.all_to_all(rows_in, 'range', split_axis=0, concat_axis=0, tiled=True)  34.8 us
    pallas_call x1, Pallas kernels, range_stage(): pl.pallas_call(kernel, grid=(steps // per_step,), in_specs=[pl.BlockSpec(...  15.4 us
    mul x1, other arithmetic, body(): sin = double(jnp.sin(theta) * scale)  13.1 us
    all_to_all x1, starting transfers between devices, body(): lax.all_to_all(blocks, ('pulse', 'range'), split_axis=0, concat_axis=0, t...  9.32 us
    pallas_call x1, Pallas kernels, azimuth_stage(): pl.pallas_call(functools.partial(azimuth_kernel, outer), grid=(count // b...  8.95 us
    broadcast_in_dim x2, local copies, waits for them, and re-layouts, body(): jnp.broadcast_to(value[:, :, None, :], (outer, LANES, 2, LANES))  8.62 us
    all_to_all x1, starting transfers between devices, body(): lax.all_to_all(rows_in, 'range', split_axis=0, concat_axis=0, tiled=True)  8.59 us
  transfers between devices with their start and end apart: 4, of which 4 were waited for; matrix products, arithmetic and copies ran while one was open for 10% of the time, Pallas kernels for 0%

commit v1 on v0

v1 whole, which is shorter than its diff:
```python
import functools
import math

import jax
import jax.numpy as jnp
import ml_dtypes
import numpy as np
from jax import lax
from jax.experimental import pallas as pl
from jax.experimental.pallas import tpu as pltpu
from jax.sharding import PartitionSpec as P


MARGIN = 512
LANES = 128
CHUNKS = 2
F32 = jnp.float32
BF16 = jnp.bfloat16


def split_const(table):
    high = table.astype(ml_dtypes.bfloat16)
    low = (table - high.astype(np.float64)).astype(ml_dtypes.bfloat16)
    return high, low


def unit_roots(rows, cols, modulus, sign):
    product = np.outer(np.arange(rows), np.arange(cols)) % modulus
    angle = sign * 2.0 * np.pi * product / modulus
    return np.cos(angle), np.sin(angle)


def dot_f32(lhs, rhs, contract):
    return lax.dot_general(lhs, rhs, (contract, ((), ())), preferred_element_type=F32)


def complex_mul(a, b):
    return a[0] * b[0] - a[1] * b[1], a[0] * b[1] + a[1] * b[0]


def by_constant(a, angle):
    cos = math.cos(angle)
    sin = math.sin(angle)
    quarter = angle / (math.pi / 2)
    if abs(quarter - round(quarter)) < 1e-9:
        turn = int(round(quarter)) % 4
        if turn == 0:
            return a
        if turn == 1:
            return -a[1], a[0]
        if turn == 2:
            return -a[0], -a[1]
        return a[1], -a[0]
    if abs(abs(cos) - abs(sin)) < 1e-9:
        half = math.sqrt(0.5)
        plus = (a[0] + a[1]) * half
        minus = (a[0] - a[1]) * half
        if cos > 0 and sin > 0:
            return minus, plus
        if cos < 0 and sin > 0:
            return -plus, minus
        if cos < 0 and sin < 0:
            return -minus, -plus
        return plus, -minus
    return a[0] * cos - a[1] * sin, a[0] * sin + a[1] * cos


def small_dft(values, sign):
    count = len(values)
    if count == 1:
        return values
    even = small_dft(values[0::2], sign)
    odd = small_dft(values[1::2], sign)
    first = []
    second = []
    for i in range(count // 2):
        turned = by_constant(odd[i], sign * 2.0 * math.pi * i / count)
        first.append((even[i][0] + turned[0], even[i][1] + turned[1]))
        second.append((even[i][0] - turned[0], even[i][1] - turned[1]))
    return first + second


def range_kernel(outer, sub, sources, shift_ref, *refs):
    echo_refs = refs[:sources]
    (twist_ref, near_ref, far_ref, phase_ref, table_ref, _, own_ref, spill_ref,
     stage_ref, mid_ref, order_ref) = refs[sources:]
    step = pl.program_id(0)
    rows = echo_refs[0].shape[1]
    inner = outer // sources
    group = 16

    @pl.when(step == 0)
    def _():
        def block(t, carry):
            at = pl.multiple_of(t * group, group)
            for n in range(inner):
                lanes = slice(n * LANES, (n + 1) * LANES)
                values = []
                for echo_ref in echo_refs:
                    values.append((
                        echo_ref[0, pl.ds(at, group), lanes].astype(F32),
                        echo_ref[1, pl.ds(at, group), lanes].astype(F32),
                    ))
                for q, value in enumerate(small_dft(values, -1.0)):
                    value = by_constant(value, -2.0 * math.pi * n * q / outer)
                    mid_ref[q, n, 0] = value[0]
                    mid_ref[q, n, 1] = value[1]
            for q in range(sources):
                values = [(mid_ref[q, n, 0], mid_ref[q, n, 1]) for n in range(inner)]
                for m, value in enumerate(small_dft(values, -1.0)):
                    stage_ref[q + sources * m, 0, pl.ds(at, group), :] = value[0]
                    stage_ref[q + sources * m, 1, pl.ds(at, group), :] = value[1]
            return carry

        lax.fori_loop(0, rows // group, block, 0)

    shift = shift_ref[0]
    per_step = phase_ref.shape[1]
    parts = []
    for i in range(per_step * sub):
        bin_low = step * per_step * sub + i
        source = lax.rem(bin_low - shift + 2 * outer, outer)
        twist = (twist_ref[0, pl.ds(bin_low, 1), :], twist_ref[1, pl.ds(bin_low, 1), :])
        value = complex_mul((stage_ref[source, 0], stage_ref[source, 1]), twist)
        parts.append(jnp.concatenate(value, axis=1).astype(BF16))
    data = jnp.concatenate(parts, axis=0)
    across = ((1,), (1,))
    product = dot_f32(table_ref[0], data, across) + dot_f32(table_ref[1], data, across)
    steps = outer // sub
    pitch = order_ref.shape[0] // LANES
    far = (far_ref[0], far_ref[1])
    for i in range(per_step):
        lanes = slice(i * LANES, (i + 1) * LANES)
        at = step * per_step + i
        near = (near_ref[0, pl.ds(at, 1), :], near_ref[1, pl.ds(at, 1), :])
        turn = complex_mul(complex_mul(far, near), (phase_ref[0, i], phase_ref[1, i]))
        real, imag = complex_mul((product[:LANES, lanes], product[LANES:, lanes]), turn)
        order_ref[pl.ds(2 * at, LANES, stride=pitch), :] = real
        order_ref[pl.ds(2 * at + 1, LANES, stride=pitch), :] = imag

    @pl.when(step == pl.num_programs(0) - 1)
    def _():
        width = 2 * steps
        owned = own_ref.shape[0] // width
        for n in range(LANES):
            value = order_ref[n * pitch:n * pitch + width, :].astype(BF16)
            if n < owned:
                own_ref[n * width:(n + 1) * width, :] = value
            else:
                spill_ref[(n - owned) * width:(n - owned + 1) * width, :] = value


def range_tables():
    cos, sin = unit_roots(LANES, LANES, LANES, -1.0)
    table = np.zeros((2, LANES, 2, LANES))
    table[0, :, 0], table[0, :, 1] = cos, -sin
    table[1, :, 0], table[1, :, 1] = sin, cos
    return np.stack(split_const(table.reshape(2 * LANES, 2 * LANES)))


def range_stage(received, twist, near, far, phase, gate, shift, outer, sub, owned_rows):
    sources = len(received)
    rows = received[0].shape[1]
    steps = outer // sub
    per_step = 2
    pitch = 2 * steps + 8
    table = range_tables()
    whole = lambda shape: pl.BlockSpec(shape, lambda i: (0,) * len(shape))
    return pl.pallas_call(
        functools.partial(range_kernel, outer, sub, sources),
        grid=(steps // per_step,),
        in_specs=[
            pl.BlockSpec(memory_space=pltpu.SMEM),
            *[whole(block.shape) for block in received],
            whole(twist.shape),
            whole(near.shape),
            whole(far.shape),
            pl.BlockSpec((2, per_step, LANES, LANES), lambda i: (0, i, 0, 0)),
            whole(table.shape),
            pl.BlockSpec(memory_space=pl.ANY),
        ],
        out_specs=[whole((2 * owned_rows, LANES)),
                   whole((2 * steps * LANES - 2 * owned_rows, LANES))],
        out_shape=[jax.ShapeDtypeStruct((2 * owned_rows, LANES), BF16),
                   jax.ShapeDtypeStruct((2 * steps * LANES - 2 * owned_rows, LANES), BF16)],
        scratch_shapes=[
            pltpu.VMEM((outer, 2, rows, LANES), F32),
            pltpu.VMEM((sources, outer // sources, 2, 16, LANES), F32),
            pltpu.VMEM((LANES * pitch, LANES), F32),
        ],
        compiler_params=pltpu.CompilerParams(
            dimension_semantics=("arbitrary",), vmem_limit_bytes=48 * 1024 * 1024),
        name="range_stage",
    )(shift, *received, twist, near, far, phase, jnp.asarray(table), gate)


def stitch_kernel(sub, limits_ref, own_ref, low_ref, high_ref, out_ref):
    side = pl.program_id(0)
    shape = own_ref.shape
    row = lax.broadcasted_iota(jnp.int32, shape, 0) // 2
    lane = lax.broadcasted_iota(jnp.int32, shape, 1)
    index = row * sub + lane // (LANES // sub)

    @pl.when(side == 0)
    def _():
        added = jnp.where(index < limits_ref[0], low_ref[...].astype(F32), 0.0)
        out_ref[...] = (own_ref[...].astype(F32) + added).astype(BF16)

    @pl.when(side == 1)
    def _():
        added = jnp.where(index >= limits_ref[1], high_ref[...].astype(F32), 0.0)
        out_ref[...] = (own_ref[...].astype(F32) + added).astype(BF16)


def stitch(own, from_below, from_above, limits, sub):
    height = from_below.shape[0]
    last = own.shape[0] // height - 1
    side = pl.BlockSpec((height, LANES), lambda i: (i * last, 0))
    whole = pl.BlockSpec((height, LANES), lambda i: (0, 0))
    return pl.pallas_call(
        functools.partial(stitch_kernel, sub),
        grid=(2,),
        in_specs=[pl.BlockSpec(memory_space=pltpu.SMEM), side, whole, whole],
        out_specs=side,
        out_shape=jax.ShapeDtypeStruct(own.shape, BF16),
        input_output_aliases={1: 0},
        compiler_params=pltpu.CompilerParams(dimension_semantics=("arbitrary",)),
        name="stitch",
    )(limits, own, from_below, from_above)


def azimuth_kernel(outer, first_ref, fore_ref, twist_ref, filter_ref, back_ref, last_ref, *refs):
    data_refs = refs[:-1]
    out_ref = refs[-1]
    chunks = len(data_refs)
    width = LANES // chunks
    count = data_refs[0].shape[0]
    twist = (twist_ref[0], twist_ref[1])
    twist_back = (twist_ref[0], -twist_ref[1])
    turn = (filter_ref[0], filter_ref[1])
    left = ((1,), (0,))
    two = lambda lhs, rhs: dot_f32(lhs[0], rhs, left) + dot_f32(lhs[1], rhs, left)
    rows = []
    for c in range(count):
        data = [ref[c] for ref in data_refs]
        spread = two((first_ref[0], first_ref[1]), jnp.concatenate(data, axis=1))
        for h in range(chunks):
            pieces = [spread[:, q * LANES + h * width:q * LANES + (h + 1) * width]
                      for q in range(chunks)]
            joined = jnp.concatenate(pieces, axis=1)
            value = complex_mul((joined[:outer], joined[outer:]), twist)
            rows.append(jnp.concatenate(value, axis=1).astype(BF16))
    total = count * chunks
    stacked = jnp.concatenate(rows, axis=0)
    doppler = dot_f32(stacked, fore_ref[0], left) + dot_f32(stacked, fore_ref[1], left)
    rows = []
    for c in range(total):
        part = doppler[c * outer:(c + 1) * outer]
        value = complex_mul((part[:, :LANES], part[:, LANES:]), turn)
        rows.append(jnp.concatenate(value, axis=1).astype(BF16))
    stacked = jnp.concatenate(rows, axis=0)
    image = dot_f32(stacked, back_ref[0], left) + dot_f32(stacked, back_ref[1], left)
    for c in range(0, total, 2):
        values = []
        for d in range(2):
            part = image[(c + d) * outer:(c + d + 1) * outer]
            value = complex_mul((part[:, :LANES], part[:, LANES:]), twist_back)
            values.append(jnp.concatenate(value, axis=0).astype(BF16))
        value = two((last_ref[0], last_ref[1]), jnp.concatenate(values, axis=1)).astype(BF16)
        out_ref[c] = value[:, :LANES]
        out_ref[c + 1] = value[:, LANES:]


def azimuth_tables(outer):
    cos, sin = unit_roots(outer, outer, outer, -1.0)
    first = np.zeros((2, outer, outer, 2))
    first[0, :, :, 0], first[0, :, :, 1] = cos, -sin
    first[1, :, :, 0], first[1, :, :, 1] = sin, cos
    last = np.zeros((outer, 2, 2, outer))
    last[:, 0, 0], last[:, 0, 1] = cos, sin
    last[:, 1, 0], last[:, 1, 1] = -sin, cos
    cos, sin = unit_roots(LANES, LANES, LANES, -1.0)
    fore = np.zeros((2, LANES, 2, LANES))
    fore[0, :, 0], fore[0, :, 1] = cos, sin
    fore[1, :, 0], fore[1, :, 1] = -sin, cos
    back = np.zeros((2, LANES, 2, LANES))
    back[0, :, 0], back[0, :, 1] = cos, -sin
    back[1, :, 0], back[1, :, 1] = sin, cos
    pair = lambda table, shape: np.stack(split_const(table.reshape(shape)))
    twist = np.stack(unit_roots(outer, LANES, outer * LANES, -1.0)).astype(np.float32)
    square = (2 * LANES, 2 * LANES)
    side = (2 * outer, 2 * outer)
    return pair(first, side), pair(fore, square), twist, pair(back, square), pair(last, side)


def azimuth_stage(data, turn, outer):
    chunks = len(data)
    count = data[0].shape[0]
    block = 8 // chunks
    first, fore, twist, back, last = azimuth_tables(outer)
    whole = lambda shape: pl.BlockSpec(shape, lambda i: (0,) * len(shape))
    tile = pl.BlockSpec((block,) + data[0].shape[1:], lambda i: (i, 0, 0))
    out_shape = (count * chunks,) + data[0].shape[1:]
    return pl.pallas_call(
        functools.partial(azimuth_kernel, outer),
        grid=(count // block,),
        in_specs=[whole(first.shape), whole(fore.shape), whole(twist.shape), whole(turn.shape),
                  whole(back.shape), whole(last.shape)] + [tile] * chunks,
        out_specs=pl.BlockSpec((block * chunks,) + out_shape[1:], lambda i: (i, 0, 0)),
        out_shape=jax.ShapeDtypeStruct(out_shape, BF16),
        compiler_params=pltpu.CompilerParams(
            dimension_semantics=("arbitrary",), vmem_limit_bytes=48 * 1024 * 1024),
        name="azimuth_stage",
    )(jnp.asarray(first), jnp.asarray(fore), jnp.asarray(twist), turn, jnp.asarray(back),
      jnp.asarray(last), *data)


def shifted(block, distance):
    devices = range(lax.axis_size("band"))
    route = [(i - distance, i) for i in devices if i - distance in devices]
    return lax.ppermute(block, "band", route)


def body(echoes, range_phase, pulse_shift, bin_offset, doppler_phase):
    range_count = lax.axis_size("range")
    group_size = lax.axis_size("pulse") * range_count
    cells_local = echoes.shape[3]
    cell_count = cells_local * range_count
    n_local = echoes.shape[2] // range_count
    spill_len = 2 * MARGIN
    owned_bins = cell_count - spill_len
    bins_local = owned_bins // group_size
    outer = cell_count // LANES
    sub = CHUNKS
    piece = n_local // sub
    steps = outer // sub
    owned_rows = owned_bins // sub

    band = lax.axis_index("band")
    bands = bin_offset.shape[0]
    order = jnp.arange(bands, dtype=jnp.int32)
    offset_of = lambda index: jnp.sum(jnp.where(order == index, bin_offset, 0))
    offset = offset_of(band)
    below = offset_of(band - 1)
    above = offset_of(band + 1)
    shift = offset - spill_len

    place = lax.axis_index("range")
    low = jnp.arange(outer, dtype=jnp.int32)
    lane = jnp.arange(LANES, dtype=jnp.int32)
    phase = jnp.concatenate((range_phase[0], range_phase[0]))
    phase = lax.dynamic_slice_in_dim(phase, spill_len - offset, cell_count, 0)
    phase = jnp.transpose(phase.reshape(LANES, steps, sub), (2, 1, 0))
    scale = 1.0 / math.sqrt(cell_count)
    phase = jnp.stack((jnp.cos(phase) * scale, jnp.sin(phase) * scale))
    cube = (2, steps, LANES, LANES)
    part = lane // piece
    spread = jnp.broadcast_to(phase[:, sub - 1][..., None], cube)
    for h in range(sub - 1):
        spread = jnp.where(part == h, phase[:, h][..., None], spread)
    low_bin = jnp.arange(steps, dtype=jnp.int32)[:, None] * sub + part - shift

    def ramp(product):
        angle = jnp.mod(product, cell_count).astype(F32) * (-2.0 * math.pi / cell_count)
        return jnp.stack((jnp.cos(angle), jnp.sin(angle)))

    doppler = jnp.transpose(doppler_phase.reshape(LANES, group_size))
    factor = 1.0 / doppler_phase.shape[0]
    turn = jnp.stack((jnp.cos(doppler) * factor, jnp.sin(doppler) * factor))

    received = []
    for q in range(sub):
        blocks = []
        for d in range(range_count):
            begin = jnp.mod(place + d, range_count) * n_local + q * piece
            block = lax.dynamic_slice_in_dim(echoes[0], begin, piece, 1)
            if d:
                route = [(i, (i + d) % range_count) for i in range(range_count)]
                block = lax.ppermute(block, "range", route)
            blocks.append(block)
        received.append([blocks[(-z) % range_count] for z in range(range_count)])

    twist = ramp((low[:, None] - shift) * (lane[None, :] + cells_local * place))
    limits = jnp.stack((below, above))
    samples = []
    gate = None
    for q in range(sub):
        shifts = jnp.tile(pulse_shift[0, q * piece:(q + 1) * piece], sub)
        near = ramp(low_bin * shifts)
        far = ramp(outer * lane[:, None] * shifts)
        gate = twist if gate is None else gate
        own, spill = range_stage(received[q], twist, near, far, spread, gate,
                                 shift.reshape(1), outer, sub, owned_rows)
        from_below = shifted(spill, 1)
        from_above = shifted(spill, -1)
        gate = stitch(own, from_below, from_above, limits, sub)
        blocks = gate.reshape(group_size, bins_local // sub, 2, LANES)
        block = lax.all_to_all(
            blocks, ("pulse", "range"), split_axis=0, concat_axis=0, tiled=True)
        samples.append(jnp.transpose(block, (1, 0, 2, 3)).reshape(
            bins_local // sub, 2 * group_size, LANES))

    image = azimuth_stage(samples, turn, group_size)
    image = jnp.transpose(image.reshape(bins_local, group_size, 2, LANES), (0, 2, 1, 3))
    return image.reshape(bins_local, 2, group_size * LANES)


def solution(mesh):
    in_specs = (
        P("band", None, "pulse", "range"),
        P("band", None),
        P("band", ("pulse", "range")),
        P(),
        P(),
    )
    out_specs = P(("band", "pulse", "range"), None, None)
    return jax.shard_map(
        body, mesh=mesh, in_specs=in_specs, out_specs=out_specs, check_vma=False)
```

time: 166 us -> 171 us (1.030)
  starting transfers between devices: 23.8 us -> 51.8 us
  waiting for transfers between devices: 81.6 us -> 66.4 us
  Pallas kernels: 24.3 us -> 19.7 us
  other arithmetic: 16.3 us -> 12.1 us
    all_to_all x1 -> x0, waiting for transfers between devices: 34.8 us -> none  [body(): lax.all_to_all(rows_in, 'range', split_axis=0, concat_axis=0, tiled=True)]
    ppermute x0 -> x6, waiting for transfers between devices: none -> 34.5 us  [body(): block = lax.ppermute(block, 'range', route)]
    all_to_all x1 -> x2, waiting for transfers between devices: 39.8 us -> 21 us  [body(): lax.all_to_all(blocks, ('pulse', 'range'), split_axis=0, concat_axis=0, t...]
    ppermute x0 -> x6, starting transfers between devices: none -> 18.5 us  [body(): block = lax.ppermute(block, 'range', route)]
    mul x2 -> x3, other arithmetic: 13.1 us -> 0.21 us  [the longest x1 0.21 us: body(): phase = jnp.stack((jnp.cos(phase) * scale, jnp.sin(phase) * scale))]
    all_to_all x1 -> x2, starting transfers between devices: 9.32 us -> 21.4 us  [body(): lax.all_to_all(blocks, ('pulse', 'range'), split_axis=0, concat_axis=0, t...]
    broadcast_in_dim x2 -> x0, local copies, waits for them, and re-layouts: 8.62 us -> none  [body(): jnp.broadcast_to(value[:, :, None, :], (outer, LANES, 2, LANES))]
    all_to_all x1 -> x0, starting transfers between devices: 8.59 us -> none  [body(): lax.all_to_all(rows_in, 'range', split_axis=0, concat_axis=0, tiled=True)]
  transfers between devices with their start and end apart: 4 -> 12, of which waited for: 4 -> 9; matrix products, arithmetic and copies ran while one was open for 10% -> 13% of each run, Pallas kernels for 0% -> 3%
where the time goes in v1:
time: 171 us; the launch traced here: 169 us
  waiting for transfers between devices  66.4 us (39%)
  starting transfers between devices  51.8 us (30%)
  Pallas kernels  19.7 us (12%)
  local copies, waits for them, and re-layouts  16.4 us (10%)
  other arithmetic  12.1 us (7%)
  between operations  2.38 us (1%)
    ppermute x6, waiting for transfers between devices, body(): block = lax.ppermute(block, 'range', route)  34.5 us
    all_to_all x2, starting transfers between devices, body(): lax.all_to_all(blocks, ('pulse', 'range'), split_axis=0, concat_axis=0, t...  21.4 us
    all_to_all x2, waiting for transfers between devices, body(): lax.all_to_all(blocks, ('pulse', 'range'), split_axis=0, concat_axis=0, t...  21 us
    ppermute x6, starting transfers between devices, body(): block = lax.ppermute(block, 'range', route)  18.5 us
    ppermute x4, starting transfers between devices, shifted(): return lax.ppermute(block, 'band', route)  11.8 us
    ppermute x4, waiting for transfers between devices, shifted(): return lax.ppermute(block, 'band', route)  10.8 us
    pallas_call x2, Pallas kernels, range_stage(): pl.pallas_call(functools.partial(range_kernel, outer, sub, sources), grid...  7.72 us
    pallas_call x1, Pallas kernels, azimuth_stage(): pl.pallas_call(functools.partial(azimuth_kernel, outer), grid=(count // b...  7.59 us
  transfers between devices with their start and end apart: 12, of which 9 were waited for; matrix products, arithmetic and copies ran while one was open for 13% of the time, Pallas kernels for 3%

profile of v1, /device:TPU:2, one launch (start us, length us, event | category | flops | bytes accessed | tf_op | source)
XLA Modules:
  0.0 168.8 jit_solution(3639686615765027910)
XLA Ops:
  0.0 2.7 %dynamic-slice_bitcast_fusion = (bf16[2,64,1024]{2,1,0:T(8,128)(2,1)}, bf16[2,64,1024]{2,1,0:T(8,128)(2,1)}, bf16[2,64,1024]{2,1,0:T(8,128)(2,1)S(1)}, bf16[2,64...) fusion(bf16[1,2,512,1024]{3,2,1,0:T(8,128)(2,1)} %param.12, ...), kind=kLoop, calls=%fused_computation.3 | loop fusion | bytes 4194336 | tf_op jit(solution)/shard_map/dynamic_slice | solution.py:376
  2.7 6.3 %collective-permute-start = (bf16[2,64,1024]{2,1,0:T(8,128)(2,1)}, bf16[2,64,1024]{2,1,0:T(8,128)(2,1)S(1)}, u32[]{:S(2)}, u32[]{:S(2)}) collective-permute-start(bf16[2,64,1024]{2,1,0:T(8,128)(2,1)} %get-tuple-element.21), channel_id=1, source_target_pairs={{0,3},{1,0},{2,1},{3,2},{4,7},{5,4},{6,5},{7,6},{8,11},{9,8},{10,9... | collective-permute-start | bytes 786440 | tf_op jit(solution)/shard_map/ppermute | solution.py:379
  10.0 2.9 %collective-permute-start.2 = (bf16[2,64,1024]{2,1,0:T(8,128)(2,1)}, bf16[2,64,1024]{2,1,0:T(8,128)(2,1)}, u32[]{:S(2)}, u32[]{:S(2)}) collective-permute-start(bf16[2,64,1024]{2,1,0:T(8,128)(2,1)} %get-tuple-element.19), channel_id=1, source_target_pairs={{0,1},{1,2},{2,3},{3,0},{4,5},{5,6},{6,7},{7,4},{8,9},{9,10},{10,1... | collective-permute-start | bytes 786440 | tf_op jit(solution)/shard_map/ppermute | solution.py:379
  15.8 2.0 %mul.288 = f32[128,16,2]{2,1,0:T(8,128)} reshape(f32[4096]{0:T(1024)S(1)} %get-tuple-element.28) | data formatting | bytes 32768 | tf_op jit(solution)/shard_map/mul | solution.py:355
  17.8 2.0 %mul.291 = f32[128,16,2]{2,1,0:T(8,128)} reshape(f32[4096]{0:T(1024)S(1)} %get-tuple-element.29) | data formatting | bytes 32768 | tf_op jit(solution)/shard_map/mul | solution.py:355
  19.7 4.3 %slice_maximum_fusion = (f32[2,1,16,128]{1,2,3,0:T(8,128)}, f32[2,1,16,128]{1,2,3,0:T(8,128)S(1)}) fusion(f32[1,2,16,128]{1,2,3,0:T(8,128)} %bitcast.54, f32[1,2,16,128]{1,2,3,0:T(8,128)} %bitcast.53), kind=kLoop, calls=%fused_computation.1 | loop fusion | flops 8192 | bytes 65536 | tf_op jit(solution)/shard_map/stack | solution.py:355
  24.1 2.4 %copy.43 = f32[2,1,16,128]{3,2,0,1:T(8,128)S(1)} copy(f32[2,1,16,128]{1,2,3,0:T(8,128)} %get-tuple-element.24) | data formatting | bytes 32768 | tf_op jit(solution)/shard_map/slice | solution.py:360
  28.4 1.2 fusion.7
  29.8 1.8 %broadcast_select_fusion.refs_7_ = f32[2,16,128,128]{3,2,1,0:T(8,128)S(1)} fusion(f32[2,16,128]{2,1,0:T(8,128)S(1)} %bitcast.59, f32[2,16,128]{2,1,0:T(8,128)S(1)} %bitcast.58, pred[128]{0:T(512)(128)(4,1)} %broadcast_compare_fusion), kind=kLoop, calls=%fused_computation.2 | loop fusion | flops 524288 | bytes 2130048 | tf_op jit(solution)/shard_map/jit(_where)/select_n | solution.py:360
  31.8 4.3 %range_stage.2 = (bf16[3072,128]{1,0:T(8,128)(2,1)S(1)}, bf16[1024,128]{1,0:T(8,128)(2,1)S(1)}) custom-call(s32[1]{0:T(128)} %bitcast.6.shift_ref, bf16[2,64,1024]{2,1,0:T(8,128)(2,1)S(1)} %get-tuple-element.22.refs_0_, bf16[2,64,1024]{2,1,0:T(8,128)(2,1)S(1)} %collective-permute-done.refs_1_, bf16[2,64,1024]{2,1,0:T(8,128)(2,1)S(1)} %collective-permute-done.1.refs_2_, ...), custom_call_target="tpu_custom_call" | custom-call | tf_op jit(solution)/shard_map/range_stage/pallas_call | solution.py:169
  37.0 3.4 %collective-permute-start.3 = (bf16[1024,128]{1,0:T(8,128)(2,1)S(1)}, bf16[1024,128]{1,0:T(8,128)(2,1)S(1)}, u32[]{:S(2)}, u32[]{:S(2)}) collective-permute-start(bf16[1024,128]{1,0:T(8,128)(2,1)S(1)} %get-tuple-element.10), channel_id=1, source_target_pairs={{0,64},{64,128},{128,192},{1,65},{65,129},{129,193},{2,66},{66,130... | collective-permute-start | bytes 786440 | tf_op jit(solution)/shard_map/ppermute | solution.py:321
  40.4 2.5 %collective-permute-start.4 = (bf16[1024,128]{1,0:T(8,128)(2,1)S(1)}, bf16[1024,128]{1,0:T(8,128)(2,1)S(1)}, u32[]{:S(2)}, u32[]{:S(2)}) collective-permute-start(bf16[1024,128]{1,0:T(8,128)(2,1)S(1)} %get-tuple-element.10), channel_id=1, source_target_pairs={{64,0},{128,64},{192,128},{65,1},{129,65},{193,129},{66,2},{130,66... | collective-permute-start | bytes 786440 | tf_op jit(solution)/shard_map/ppermute | solution.py:321
  42.9 1.9 %pad_add_fusion.limits_ref = s32[2]{0:T(128)} fusion(s32[1]{0:T(128)} %bitcast.5, s32[1]{0:T(128)} %bitcast.4), kind=kLoop, calls=%fused_computation.81 | loop fusion | flops 2 | bytes 16 | tf_op jit(solution)/shard_map/stack | solution.py:384
  45.9 3.1 %collective-permute-done.4.high_ref = bf16[1024,128]{1,0:T(8,128)(2,1)S(1)} collective-permute-done((bf16[1024,128]{1,0:T(8,128)(2,1)S(1)}, bf16[1024,128]{1,0:T(8,128)(2,1)S(1)}, u32[]{:S(2)}, u32[]{:S(2)}) %collective-permute-start.4) | collective-permute-done | bytes 262176 | tf_op jit(solution)/shard_map/ppermute | solution.py:321
  49.8 2.2 %stitch.2.refs_9_ = bf16[3072,128]{1,0:T(8,128)(2,1)} custom-call(s32[2]{0:T(128)} %pad_add_fusion.limits_ref, bf16[3072,128]{1,0:T(8,128)(2,1)} %copy-done, bf16[1024,128]{1,0:T(8,128)(2,1)} %copy-done.8, bf16[1024,128]{1,0:T(8,128)(2,1)} %copy-done.9), custom_call_target="tpu_custom_call", output_to_operand_aliasing={{}: (1, {})} | custom-call | tf_op jit(solution)/shard_map/stitch/pallas_call | solution.py:220
  52.0 13.9 %all-to-all-start = ((bf16[64,24,2,128]{3,2,1,0:T(2,128)(2,1)}), bf16[64,24,2,128]{3,2,1,0:T(2,128)(2,1)}, u32[]{:S(2)}, u32[]{:S(2)}) async-start(bf16[64,24,2,128]{3,2,1,0:T(2,128)(2,1)} %bitcast.49), calls=%async_computation | async-start | bytes 1572864 | tf_op jit(solution)/shard_map/all_to_all | solution.py:398
  65.9 3.7 %collective-permute-start.5 = (bf16[2,64,1024]{2,1,0:T(8,128)(2,1)}, bf16[2,64,1024]{2,1,0:T(8,128)(2,1)S(1)}, u32[]{:S(2)}, u32[]{:S(2)}) collective-permute-start(bf16[2,64,1024]{2,1,0:T(8,128)(2,1)} %get-tuple-element.17), channel_id=1, source_target_pairs={{0,3},{1,0},{2,1},{3,2},{4,7},{5,4},{6,5},{7,6},{8,11},{9,8},{10,9... | collective-permute-start | bytes 786440 | tf_op jit(solution)/shard_map/ppermute | solution.py:379
  69.6 2.4 %collective-permute-start.6 = (bf16[2,64,1024]{2,1,0:T(8,128)(2,1)}, bf16[2,64,1024]{2,1,0:T(8,128)(2,1)S(1)}, u32[]{:S(2)}, u32[]{:S(2)}) collective-permute-start(bf16[2,64,1024]{2,1,0:T(8,128)(2,1)} %get-tuple-element.23), channel_id=1, source_target_pairs={{0,2},{1,3},{2,0},{3,1},{4,6},{5,7},{6,4},{7,5},{8,10},{9,11},{10,... | collective-permute-start | bytes 786440 | tf_op jit(solution)/shard_map/ppermute | solution.py:379
  71.9 2.4 %collective-permute-start.7 = (bf16[2,64,1024]{2,1,0:T(8,128)(2,1)}, bf16[2,64,1024]{2,1,0:T(8,128)(2,1)S(1)}, u32[]{:S(2)}, u32[]{:S(2)}) collective-permute-start(bf16[2,64,1024]{2,1,0:T(8,128)(2,1)} %get-tuple-element.16), channel_id=1, source_target_pairs={{0,1},{1,2},{2,3},{3,0},{4,5},{5,6},{6,7},{7,4},{8,9},{9,10},{10,1... | collective-permute-start | bytes 786440 | tf_op jit(solution)/shard_map/ppermute | solution.py:379
  75.1 23.9 %collective-permute-done.5.refs_1_ = bf16[2,64,1024]{2,1,0:T(8,128)(2,1)S(1)} collective-permute-done((bf16[2,64,1024]{2,1,0:T(8,128)(2,1)}, bf16[2,64,1024]{2,1,0:T(8,128)(2,1)S(1)}, u32[]{:S(2)}, u32[]{:S(2)}) %collective-permute-start.5) | collective-permute-done | bytes 262176 | tf_op jit(solution)/shard_map/ppermute | solution.py:379
  99.0 6.9 %collective-permute-done.6.refs_2_ = bf16[2,64,1024]{2,1,0:T(8,128)(2,1)S(1)} collective-permute-done((bf16[2,64,1024]{2,1,0:T(8,128)(2,1)}, bf16[2,64,1024]{2,1,0:T(8,128)(2,1)S(1)}, u32[]{:S(2)}, u32[]{:S(2)}) %collective-permute-start.6) | collective-permute-done | bytes 262176 | tf_op jit(solution)/shard_map/ppermute | solution.py:379
  105.9 3.5 %collective-permute-done.7.refs_3_ = bf16[2,64,1024]{2,1,0:T(8,128)(2,1)S(1)} collective-permute-done((bf16[2,64,1024]{2,1,0:T(8,128)(2,1)}, bf16[2,64,1024]{2,1,0:T(8,128)(2,1)S(1)}, u32[]{:S(2)}, u32[]{:S(2)}) %collective-permute-start.7) | collective-permute-done | bytes 262176 | tf_op jit(solution)/shard_map/ppermute | solution.py:379
  109.4 3.4 %range_stage.3 = (bf16[3072,128]{1,0:T(8,128)(2,1)S(1)}, bf16[1024,128]{1,0:T(8,128)(2,1)S(1)}) custom-call(s32[1]{0:T(128)} %bitcast.6.shift_ref, bf16[2,64,1024]{2,1,0:T(8,128)(2,1)S(1)} %get-tuple-element.18.refs_0_, bf16[2,64,1024]{2,1,0:T(8,128)(2,1)S(1)} %collective-permute-done.5.refs_1_, bf16[2,64,1024]{2,1,0:T(8,128)(2,1)S(1)} %collective-permute-done.6.refs_2_, ...), custom_call_target="tpu_custom_call" | custom-call | tf_op jit(solution)/shard_map/range_stage/pallas_call | solution.py:169
  113.8 3.2 %collective-permute-start.8 = (bf16[1024,128]{1,0:T(8,128)(2,1)S(1)}, bf16[1024,128]{1,0:T(8,128)(2,1)S(1)}, u32[]{:S(2)}, u32[]{:S(2)}) collective-permute-start(bf16[1024,128]{1,0:T(8,128)(2,1)S(1)} %get-tuple-element.12), channel_id=1, source_target_pairs={{0,64},{64,128},{128,192},{1,65},{65,129},{129,193},{2,66},{66,130... | collective-permute-start | bytes 786440 | tf_op jit(solution)/shard_map/ppermute | solution.py:321
  117.0 2.8 %collective-permute-start.9 = (bf16[1024,128]{1,0:T(8,128)(2,1)S(1)}, bf16[1024,128]{1,0:T(8,128)(2,1)S(1)}, u32[]{:S(2)}, u32[]{:S(2)}) collective-permute-start(bf16[1024,128]{1,0:T(8,128)(2,1)S(1)} %get-tuple-element.12), channel_id=1, source_target_pairs={{64,0},{128,64},{192,128},{65,1},{129,65},{193,129},{66,2},{130,66... | collective-permute-start | bytes 786440 | tf_op jit(solution)/shard_map/ppermute | solution.py:321
  119.8 3.8 %collective-permute-done.8.low_ref = bf16[1024,128]{1,0:T(8,128)(2,1)S(1)} collective-permute-done((bf16[1024,128]{1,0:T(8,128)(2,1)S(1)}, bf16[1024,128]{1,0:T(8,128)(2,1)S(1)}, u32[]{:S(2)}, u32[]{:S(2)}) %collective-permute-start.8) | collective-permute-done | bytes 262176 | tf_op jit(solution)/shard_map/ppermute | solution.py:321
  123.5 2.8 %collective-permute-done.9.high_ref = bf16[1024,128]{1,0:T(8,128)(2,1)S(1)} collective-permute-done((bf16[1024,128]{1,0:T(8,128)(2,1)S(1)}, bf16[1024,128]{1,0:T(8,128)(2,1)S(1)}, u32[]{:S(2)}, u32[]{:S(2)}) %collective-permute-start.9) | collective-permute-done | bytes 262176 | tf_op jit(solution)/shard_map/ppermute | solution.py:321
  127.1 2.2 %stitch.3 = bf16[3072,128]{1,0:T(8,128)(2,1)} custom-call(s32[2]{0:T(128)} %pad_add_fusion.limits_ref, bf16[3072,128]{1,0:T(8,128)(2,1)} %copy-done.2, bf16[1024,128]{1,0:T(8,128)(2,1)} %copy-done.10, bf16[1024,128]{1,0:T(8,128)(2,1)} %copy-done.11), custom_call_target="tpu_custom_call", output_to_operand_aliasing={{}: (1, {})} | custom-call | tf_op jit(solution)/shard_map/stitch/pallas_call | solution.py:220
  129.3 7.5 %all-to-all-start.1 = ((bf16[64,24,2,128]{3,2,1,0:T(2,128)(2,1)}), bf16[64,24,2,128]{3,2,1,0:T(2,128)(2,1)S(1)}, u32[]{:S(2)}, u32[]{:S(2)}) async-start(bf16[64,24,2,128]{3,2,1,0:T(2,128)(2,1)} %bitcast.50), calls=%async_computation.1 | async-start | bytes 1572864 | tf_op jit(solution)/shard_map/all_to_all | solution.py:398
  137.4 1.9 %copy.45 = bf16[24,64,2,128]{3,2,1,0:T(2,128)(2,1)S(1)} copy(bf16[24,64,2,128]{3,2,0,1:T(2,128)(2,1)} %bitcast.20) | data formatting | bytes 1572864 | tf_op jit(solution)/shard_map/transpose | solution.py:400
  139.3 21.0 %all-to-all-done.1 = bf16[64,24,2,128]{3,2,1,0:T(2,128)(2,1)S(1)} async-done(((bf16[64,24,2,128]{3,2,1,0:T(2,128)(2,1)}), bf16[64,24,2,128]{3,2,1,0:T(2,128)(2,1)S(1)}, u32[]{:S(2)}, u32[]{:S(2)}) %all-to-all-start.1) | async-done | bytes 786464 | tf_op jit(solution)/shard_map/all_to_all | solution.py:398
  161.2 7.6 %azimuth_stage.1 = bf16[48,128,128]{2,1,0:T(8,128)(2,1)} custom-call(bf16[2,128,128]{2,1,0:T(8,128)(2,1)S(1)} %copy-done.5, bf16[2,256,256]{2,1,0:T(8,128)(2,1)S(1)} %copy-done.4, f32[2,64,128]{2,1,0:T(8,128)S(1)} %copy-done.6, f32[2,64,128]{2,1,0:T(8,128)S(1)} %pad_maximum_fusion.3.filter_ref, bf16[2,256,256]{2,1,0:T(8,128)(2,1)S(1)} %copy-done.3, ...), custom_call_target="tpu_custom_call" | custom-call | tf_op jit(solution)/shard_map/azimuth_stage/pallas_call | solution.py:304
  (66 shorter events, 10.5 us)
Async XLA Ops:
  0.0 13.4 %copy-start.15 = (s32[4]{0:T(128)S(1)}, s32[4]{0:T(128)}, u32[]{:S(2)}) copy-start(s32[4]{0:T(128)} %param.15) | copy-start | bytes 52
  0.0 15.5 %copy-start.13 = (f32[1,4096]{1,0:T(1,128)S(1)}, f32[1,4096]{1,0:T(1,128)}, u32[]{:S(2)}) copy-start(f32[1,4096]{1,0:T(1,128)} %param.13) | copy-start | bytes 49156
  2.7 29.1 %collective-permute-start = (bf16[2,64,1024]{2,1,0:T(8,128)(2,1)}, bf16[2,64,1024]{2,1,0:T(8,128)(2,1)S(1)}, u32[]{:S(2)}, u32[]{:S(2)}) collective-permute-start(bf16[2,64,1024]{2,1,0:T(8,128)(2,1)} %get-tuple-element.21), channel_id=1, source_target_pairs={{0,3},{1,0},{2,1},{3,2},{4,7},{5,4},{6,5},{7,6},{8,11},{9,8},{10,9... | collective-permute-start | bytes 786440 | tf_op jit(solution)/shard_map/ppermute | solution.py:379
  9.0 22.8 %collective-permute-start.1 = (bf16[2,64,1024]{2,1,0:T(8,128)(2,1)}, bf16[2,64,1024]{2,1,0:T(8,128)(2,1)S(1)}, u32[]{:S(2)}, u32[]{:S(2)}) collective-permute-start(bf16[2,64,1024]{2,1,0:T(8,128)(2,1)} %get-tuple-element.20), channel_id=1, source_target_pairs={{0,2},{1,3},{2,0},{3,1},{4,6},{5,7},{6,4},{7,5},{8,10},{9,11},{10,... | collective-permute-start | bytes 786440 | tf_op jit(solution)/shard_map/ppermute | solution.py:379
  10.0 21.8 %collective-permute-start.2 = (bf16[2,64,1024]{2,1,0:T(8,128)(2,1)}, bf16[2,64,1024]{2,1,0:T(8,128)(2,1)}, u32[]{:S(2)}, u32[]{:S(2)}) collective-permute-start(bf16[2,64,1024]{2,1,0:T(8,128)(2,1)} %get-tuple-element.19), channel_id=1, source_target_pairs={{0,1},{1,2},{2,3},{3,0},{4,5},{5,6},{6,7},{7,4},{8,9},{9,10},{10,1... | collective-permute-start | bytes 786440 | tf_op jit(solution)/shard_map/ppermute | solution.py:379
  24.1 3.9 %copy-start.14 = (s32[1,128]{1,0:T(1,128)S(1)}, s32[1,128]{1,0:T(1,128)}, u32[]{:S(2)}) copy-start(s32[1,128]{1,0:T(1,128)} %param.14) | copy-start | bytes 1540
  26.4 5.4 %copy-start.3 = (bf16[2,256,256]{2,1,0:T(8,128)(2,1)S(1)}, bf16[2,256,256]{2,1,0:T(8,128)(2,1)}, u32[]{:S(2)}) copy-start(bf16[2,256,256]{2,1,0:T(8,128)(2,1)} %constant.153.clone.refs_8_.back_ref) | copy-start | bytes 786436
  36.1 0.9 copy-start
  37.0 8.9 %collective-permute-start.3 = (bf16[1024,128]{1,0:T(8,128)(2,1)S(1)}, bf16[1024,128]{1,0:T(8,128)(2,1)S(1)}, u32[]{:S(2)}, u32[]{:S(2)}) collective-permute-start(bf16[1024,128]{1,0:T(8,128)(2,1)S(1)} %get-tuple-element.10), channel_id=1, source_target_pairs={{0,64},{64,128},{128,192},{1,65},{65,129},{129,193},{2,66},{66,130... | collective-permute-start | bytes 786440 | tf_op jit(solution)/shard_map/ppermute | solution.py:321
  40.4 8.6 %collective-permute-start.4 = (bf16[1024,128]{1,0:T(8,128)(2,1)S(1)}, bf16[1024,128]{1,0:T(8,128)(2,1)S(1)}, u32[]{:S(2)}, u32[]{:S(2)}) collective-permute-start(bf16[1024,128]{1,0:T(8,128)(2,1)S(1)} %get-tuple-element.10), channel_id=1, source_target_pairs={{64,0},{128,64},{192,128},{65,1},{129,65},{193,129},{66,2},{130,66... | collective-permute-start | bytes 786440 | tf_op jit(solution)/shard_map/ppermute | solution.py:321
  45.9 3.1 %copy-start.8 = (bf16[1024,128]{1,0:T(8,128)(2,1)}, bf16[1024,128]{1,0:T(8,128)(2,1)S(1)}, u32[]{:S(2)}) copy-start(bf16[1024,128]{1,0:T(8,128)(2,1)S(1)} %collective-permute-done.3.low_ref) | copy-start | bytes 786436
  49.1 0.7 copy-start.9
  52.0 57.5 %copy-start.1 = (bf16[3072,128]{1,0:T(8,128)(2,1)S(1)}, bf16[3072,128]{1,0:T(8,128)(2,1)}, u32[]{:S(2)}) copy-start(bf16[3072,128]{1,0:T(8,128)(2,1)} %stitch.2.refs_9_) | copy-start | bytes 2359300
  52.0 77.3 %all-to-all-start = ((bf16[64,24,2,128]{3,2,1,0:T(2,128)(2,1)}), bf16[64,24,2,128]{3,2,1,0:T(2,128)(2,1)}, u32[]{:S(2)}, u32[]{:S(2)}) async-start(bf16[64,24,2,128]{3,2,1,0:T(2,128)(2,1)} %bitcast.49), calls=%async_computation | async-start | bytes 1572864 | tf_op jit(solution)/shard_map/all_to_all | solution.py:398
  65.9 33.1 %collective-permute-start.5 = (bf16[2,64,1024]{2,1,0:T(8,128)(2,1)}, bf16[2,64,1024]{2,1,0:T(8,128)(2,1)S(1)}, u32[]{:S(2)}, u32[]{:S(2)}) collective-permute-start(bf16[2,64,1024]{2,1,0:T(8,128)(2,1)} %get-tuple-element.17), channel_id=1, source_target_pairs={{0,3},{1,0},{2,1},{3,2},{4,7},{5,4},{6,5},{7,6},{8,11},{9,8},{10,9... | collective-permute-start | bytes 786440 | tf_op jit(solution)/shard_map/ppermute | solution.py:379
  69.6 36.4 %collective-permute-start.6 = (bf16[2,64,1024]{2,1,0:T(8,128)(2,1)}, bf16[2,64,1024]{2,1,0:T(8,128)(2,1)S(1)}, u32[]{:S(2)}, u32[]{:S(2)}) collective-permute-start(bf16[2,64,1024]{2,1,0:T(8,128)(2,1)} %get-tuple-element.23), channel_id=1, source_target_pairs={{0,2},{1,3},{2,0},{3,1},{4,6},{5,7},{6,4},{7,5},{8,10},{9,11},{10,... | collective-permute-start | bytes 786440 | tf_op jit(solution)/shard_map/ppermute | solution.py:379
  71.9 37.5 %collective-permute-start.7 = (bf16[2,64,1024]{2,1,0:T(8,128)(2,1)}, bf16[2,64,1024]{2,1,0:T(8,128)(2,1)S(1)}, u32[]{:S(2)}, u32[]{:S(2)}) collective-permute-start(bf16[2,64,1024]{2,1,0:T(8,128)(2,1)} %get-tuple-element.16), channel_id=1, source_target_pairs={{0,1},{1,2},{2,3},{3,0},{4,5},{5,6},{6,7},{7,4},{8,9},{9,10},{10,1... | collective-permute-start | bytes 786440 | tf_op jit(solution)/shard_map/ppermute | solution.py:379
  112.8 0.9 copy-start.2
  113.8 23.1 %copy-start.12 = (f32[8192]{0:T(1024)S(1)}, f32[8192]{0:T(1024)}, u32[]{:S(2)}) copy-start(f32[8192]{0:T(1024)} %param.16) | copy-start | bytes 98308
  113.8 9.8 %collective-permute-start.8 = (bf16[1024,128]{1,0:T(8,128)(2,1)S(1)}, bf16[1024,128]{1,0:T(8,128)(2,1)S(1)}, u32[]{:S(2)}, u32[]{:S(2)}) collective-permute-start(bf16[1024,128]{1,0:T(8,128)(2,1)S(1)} %get-tuple-element.12), channel_id=1, source_target_pairs={{0,64},{64,128},{128,192},{1,65},{65,129},{129,193},{2,66},{66,130... | collective-permute-start | bytes 786440 | tf_op jit(solution)/shard_map/ppermute | solution.py:321
  117.0 9.4 %collective-permute-start.9 = (bf16[1024,128]{1,0:T(8,128)(2,1)S(1)}, bf16[1024,128]{1,0:T(8,128)(2,1)S(1)}, u32[]{:S(2)}, u32[]{:S(2)}) collective-permute-start(bf16[1024,128]{1,0:T(8,128)(2,1)S(1)} %get-tuple-element.12), channel_id=1, source_target_pairs={{64,0},{128,64},{192,128},{65,1},{129,65},{193,129},{66,2},{130,66... | collective-permute-start | bytes 786440 | tf_op jit(solution)/shard_map/ppermute | solution.py:321
  123.5 2.8 %copy-start.10 = (bf16[1024,128]{1,0:T(8,128)(2,1)}, bf16[1024,128]{1,0:T(8,128)(2,1)S(1)}, u32[]{:S(2)}) copy-start(bf16[1024,128]{1,0:T(8,128)(2,1)S(1)} %collective-permute-done.8.low_ref) | copy-start | bytes 786436
  126.4 0.7 copy-start.11
  129.3 31.1 %all-to-all-start.1 = ((bf16[64,24,2,128]{3,2,1,0:T(2,128)(2,1)}), bf16[64,24,2,128]{3,2,1,0:T(2,128)(2,1)S(1)}, u32[]{:S(2)}, u32[]{:S(2)}) async-start(bf16[64,24,2,128]{3,2,1,0:T(2,128)(2,1)} %bitcast.50), calls=%async_computation.1 | async-start | bytes 1572864 | tf_op jit(solution)/shard_map/all_to_all | solution.py:398
  136.9 24.3 %copy-start.4 = (bf16[2,256,256]{2,1,0:T(8,128)(2,1)S(1)}, bf16[2,256,256]{2,1,0:T(8,128)(2,1)}, u32[]{:S(2)}) copy-start(bf16[2,256,256]{2,1,0:T(8,128)(2,1)} %constant.155.clone.fore_ref) | copy-start | bytes 786436
  136.9 24.3 %copy-start.5 = (bf16[2,128,128]{2,1,0:T(8,128)(2,1)S(1)}, bf16[2,128,128]{2,1,0:T(8,128)(2,1)}, u32[]{:S(2)}) copy-start(bf16[2,128,128]{2,1,0:T(8,128)(2,1)} %constant.154.clone.first_ref) | copy-start | bytes 196612
  136.9 24.3 %copy-start.6 = (f32[2,64,128]{2,1,0:T(8,128)S(1)}, f32[2,64,128]{2,1,0:T(8,128)}, u32[]{:S(2)}) copy-start(f32[2,64,128]{2,1,0:T(8,128)} %constant.156.clone.twist_ref) | copy-start | bytes 196612
  136.9 24.3 %copy-start.7 = (bf16[2,128,128]{2,1,0:T(8,128)(2,1)S(1)}, bf16[2,128,128]{2,1,0:T(8,128)(2,1)}, u32[]{:S(2)}) copy-start(bf16[2,128,128]{2,1,0:T(8,128)(2,1)} %constant.157.clone.last_ref) | copy-start | bytes 196612

commit v2 on v1

--- a/solution.py
+++ b/solution.py
@@ -80,10 +80,10 @@
     return first + second
 
 
-def range_kernel(outer, sub, sources, shift_ref, *refs):
-    echo_refs = refs[:sources]
+def range_kernel(outer, sub, sources, scalar_ref, mine_ref, *refs):
+    echo_refs = (mine_ref,) + refs[:sources - 1]
     (twist_ref, near_ref, far_ref, phase_ref, table_ref, _, own_ref, spill_ref,
-     stage_ref, mid_ref, order_ref) = refs[sources:]
+     stage_ref, mid_ref, order_ref) = refs[sources - 1:]
     step = pl.program_id(0)
     rows = echo_refs[0].shape[1]
     inner = outer // sources
@@ -114,7 +114,7 @@
 
         lax.fori_loop(0, rows // group, block, 0)
 
-    shift = shift_ref[0]
+    shift = scalar_ref[0]
     per_step = phase_ref.shape[1]
     parts = []
     for i in range(per_step * sub):
@@ -158,75 +158,95 @@
     return np.stack(split_const(table.reshape(2 * LANES, 2 * LANES)))
 
 
-def range_stage(received, twist, near, far, phase, gate, shift, outer, sub, owned_rows):
-    sources = len(received)
-    rows = received[0].shape[1]
+def range_stage(scalars, echoes, chunk, received, twist, near, far, phase, gate, sub, owned_rows):
+    sources = len(received) + 1
+    outer = twist.shape[1]
     steps = outer // sub
     per_step = 2
     pitch = 2 * steps + 8
     table = range_tables()
-    whole = lambda shape: pl.BlockSpec(shape, lambda i: (0,) * len(shape))
+    rows = echoes.shape[3]
+    whole = lambda shape: pl.BlockSpec(shape, lambda i, s: (0,) * len(shape))
+    mine = pl.BlockSpec((2, None, None) + echoes.shape[3:], lambda i, s: (0, s[1], chunk, 0, 0))
+    spill_rows = steps * LANES - owned_rows
     return pl.pallas_call(
         functools.partial(range_kernel, outer, sub, sources),
-        grid=(steps // per_step,),
-        in_specs=[
-            pl.BlockSpec(memory_space=pltpu.SMEM),
-            *[whole(block.shape) for block in received],
-            whole(twist.shape),
-            whole(near.shape),
-            whole(far.shape),
-            pl.BlockSpec((2, per_step, LANES, LANES), lambda i: (0, i, 0, 0)),
-            whole(table.shape),
-            pl.BlockSpec(memory_space=pl.ANY),
-        ],
-        out_specs=[whole((2 * owned_rows, LANES)),
-                   whole((2 * steps * LANES - 2 * owned_rows, LANES))],
+        grid_spec=pltpu.PrefetchScalarGridSpec(
+            num_scalar_prefetch=1,
+            grid=(steps // per_step,),
+            in_specs=[
+                mine,
+                *[whole(block.shape) for block in received],
+                whole(twist.shape),
+                whole(near.shape),
+                whole(far.shape),
+                pl.BlockSpec((2, per_step, LANES, LANES), lambda i, s: (0, i, 0, 0)),
+                whole(table.shape),
+                pl.BlockSpec(memory_space=pl.ANY),
+            ],
+            out_specs=[whole((2 * owned_rows, LANES)), whole((2 * spill_rows, LANES))],
+            scratch_shapes=[
+                pltpu.VMEM((outer, 2, rows, LANES), F32),
+                pltpu.VMEM((sources, outer // sources, 2, 16, LANES), F32),
+                pltpu.VMEM((LANES * pitch, LANES), F32),
+            ],
+        ),
         out_shape=[jax.ShapeDtypeStruct((2 * owned_rows, LANES), BF16),
-                   jax.ShapeDtypeStruct((2 * steps * LANES - 2 * owned_rows, LANES), BF16)],
-        scratch_shapes=[
-            pltpu.VMEM((outer, 2, rows, LANES), F32),
-            pltpu.VMEM((sources, outer // sources, 2, 16, LANES), F32),
-            pltpu.VMEM((LANES * pitch, LANES), F32),
-        ],
+                   jax.ShapeDtypeStruct((2 * spill_rows, LANES), BF16)],
         compiler_params=pltpu.CompilerParams(
-            dimension_semantics=("arbitrary",), vmem_limit_bytes=48 * 1024 * 1024),
+            dimension_semantics=("arbitrary",), vmem_limit_bytes=16 * 1024 * 1024),
         name="range_stage",
-    )(shift, *received, twist, near, far, phase, jnp.asarray(table), gate)
-
-
-def stitch_kernel(sub, limits_ref, own_ref, low_ref, high_ref, out_ref):
-    side = pl.program_id(0)
+    )(scalars, echoes, *received, twist, near, far, phase, jnp.asarray(table), gate)
+
+
+def stitch_kernel(sub, edge, scalar_ref, own_ref, low_ref, high_ref, out_ref):
+    step = pl.program_id(0)
+    count = pl.num_programs(0)
     shape = own_ref.shape
-    row = lax.broadcasted_iota(jnp.int32, shape, 0) // 2
     lane = lax.broadcasted_iota(jnp.int32, shape, 1)
-    index = row * sub + lane // (LANES // sub)
-
-    @pl.when(side == 0)
+    row = lax.broadcasted_iota(jnp.int32, shape, 0)
+    index = row // 2 * sub + lane // (LANES // sub)
+    per_step = shape[0] // 2 * sub
+
+    @pl.when(step < edge)
     def _():
-        added = jnp.where(index < limits_ref[0], low_ref[...].astype(F32), 0.0)
+        keep = index < scalar_ref[2] - step * per_step
+        added = jnp.where(keep, low_ref[...].astype(F32), 0.0)
         out_ref[...] = (own_ref[...].astype(F32) + added).astype(BF16)
 
-    @pl.when(side == 1)
+    @pl.when(jnp.logical_and(step >= edge, step < count - edge))
     def _():
-        added = jnp.where(index >= limits_ref[1], high_ref[...].astype(F32), 0.0)
+        out_ref[...] = own_ref[...]
+
+    @pl.when(step >= count - edge)
+    def _():
+        keep = index >= scalar_ref[3] - (step - (count - edge)) * per_step
+        added = jnp.where(keep, high_ref[...].astype(F32), 0.0)
         out_ref[...] = (own_ref[...].astype(F32) + added).astype(BF16)
 
 
-def stitch(own, from_below, from_above, limits, sub):
-    height = from_below.shape[0]
-    last = own.shape[0] // height - 1
-    side = pl.BlockSpec((height, LANES), lambda i: (i * last, 0))
-    whole = pl.BlockSpec((height, LANES), lambda i: (0, 0))
+def stitch(scalars, own, from_below, from_above, sub):
+    edge = 1
+    height = from_below.shape[0] // edge
+    count = own.shape[0] // height
+    tile = lambda index: pl.BlockSpec((height, LANES), index)
     return pl.pallas_call(
-        functools.partial(stitch_kernel, sub),
-        grid=(2,),
-        in_specs=[pl.BlockSpec(memory_space=pltpu.SMEM), side, whole, whole],
-        out_specs=side,
+        functools.partial(stitch_kernel, sub, edge),
+        grid_spec=pltpu.PrefetchScalarGridSpec(
+            num_scalar_prefetch=1,
+            grid=(count,),
+            in_specs=[
+                tile(lambda i, s: (i, 0)),
+                tile(lambda i, s: (jnp.minimum(i, edge - 1), 0)),
+                tile(lambda i, s: (jnp.maximum(i - (count - edge), 0), 0)),
+            ],
+            out_specs=tile(lambda i, s: (i, 0)),
+        ),
         out_shape=jax.ShapeDtypeStruct(own.shape, BF16),
-        input_output_aliases={1: 0},
-        compiler_params=pltpu.CompilerParams(dimension_semantics=("arbitrary",)),
+        compiler_params=pltpu.CompilerParams(
+            dimension_semantics=("arbitrary",), vmem_limit_bytes=8 * 1024 * 1024),
         name="stitch",
-    )(limits, own, from_below, from_above)
+    )(scalars, own, from_below, from_above)
 
 
 def azimuth_kernel(outer, first_ref, fore_ref, twist_ref, filter_ref, back_ref, last_ref, *refs):
@@ -309,7 +329,7 @@
         out_specs=pl.BlockSpec((block * chunks,) + out_shape[1:], lambda i: (i, 0, 0)),
         out_shape=jax.ShapeDtypeStruct(out_shape, BF16),
         compiler_params=pltpu.CompilerParams(
-            dimension_semantics=("arbitrary",), vmem_limit_bytes=48 * 1024 * 1024),
+            dimension_semantics=("arbitrary",), vmem_limit_bytes=16 * 1024 * 1024),
         name="azimuth_stage",
     )(jnp.asarray(first), jnp.asarray(fore), jnp.asarray(twist), turn, jnp.asarray(back),
       jnp.asarray(last), *data)
@@ -350,14 +370,18 @@
     lane = jnp.arange(LANES, dtype=jnp.int32)
     phase = jnp.concatenate((range_phase[0], range_phase[0]))
     phase = lax.dynamic_slice_in_dim(phase, spill_len - offset, cell_count, 0)
-    phase = jnp.transpose(phase.reshape(LANES, steps, sub), (2, 1, 0))
+    phase = lax.optimization_barrier(jnp.transpose(phase.reshape(LANES, outer)))
     scale = 1.0 / math.sqrt(cell_count)
-    phase = jnp.stack((jnp.cos(phase) * scale, jnp.sin(phase) * scale))
-    cube = (2, steps, LANES, LANES)
+    phase = phase.reshape(steps, sub, LANES)
     part = lane // piece
-    spread = jnp.broadcast_to(phase[:, sub - 1][..., None], cube)
-    for h in range(sub - 1):
-        spread = jnp.where(part == h, phase[:, h][..., None], spread)
+    cube = (steps, LANES, LANES)
+    spread = []
+    for value in (jnp.cos(phase) * scale, jnp.sin(phase) * scale):
+        wide = jnp.broadcast_to(value[:, sub - 1][..., None], cube)
+        for h in range(sub - 1):
+            wide = jnp.where(part == h, value[:, h][..., None], wide)
+        spread.append(wide)
+    spread = jnp.stack(spread)
     low_bin = jnp.arange(steps, dtype=jnp.int32)[:, None] * sub + part - shift
 
     def ramp(product):
@@ -369,19 +393,20 @@
     turn = jnp.stack((jnp.cos(doppler) * factor, jnp.sin(doppler) * factor))
 
     received = []
+    source = echoes[0]
     for q in range(sub):
         blocks = []
-        for d in range(range_count):
+        for d in range(1, range_count):
             begin = jnp.mod(place + d, range_count) * n_local + q * piece
-            block = lax.dynamic_slice_in_dim(echoes[0], begin, piece, 1)
-            if d:
-                route = [(i, (i + d) % range_count) for i in range(range_count)]
-                block = lax.ppermute(block, "range", route)
-            blocks.append(block)
-        received.append([blocks[(-z) % range_count] for z in range(range_count)])
+            block = lax.dynamic_slice_in_dim(source, begin, piece, 1)
+            route = [(i, (i + d) % range_count) for i in range(range_count)]
+            blocks.append(lax.ppermute(block, "range", route))
+        received.append(blocks[::-1])
+        source = lax.optimization_barrier(source)
+    held = echoes[0].reshape(2, range_count, sub, piece, cells_local)
+    scalars = jnp.stack((shift, place, below, above))
 
     twist = ramp((low[:, None] - shift) * (lane[None, :] + cells_local * place))
-    limits = jnp.stack((below, above))
     samples = []
     gate = None
     for q in range(sub):
@@ -389,11 +414,11 @@
         near = ramp(low_bin * shifts)
         far = ramp(outer * lane[:, None] * shifts)
         gate = twist if gate is None else gate
-        own, spill = range_stage(received[q], twist, near, far, spread, gate,
-                                 shift.reshape(1), outer, sub, owned_rows)
+        own, spill = range_stage(scalars, held, q, received[q], twist, near, far, spread,
+                                 gate, sub, owned_rows)
         from_below = shifted(spill, 1)
         from_above = shifted(spill, -1)
-        gate = stitch(own, from_below, from_above, limits, sub)
+        gate = stitch(scalars, own, from_below, from_above, sub)
         blocks = gate.reshape(group_size, bins_local // sub, 2, LANES)
         block = lax.all_to_all(
             blocks, ("pulse", "range"), split_axis=0, concat_axis=0, tiled=True)

time: 171 us -> 169 us (0.988)
  waiting for transfers between devices: 66.4 us -> 78 us
  local copies, waits for them, and re-layouts: 16.4 us -> 7.79 us
  other arithmetic: 12.1 us -> 6.71 us
    ppermute x6, waiting for transfers between devices: 34.5 us -> 43.4 us  [body(): blocks.append(lax.ppermute(block, 'range', route))]
    another operation x2, other arithmetic: 6.28 us -> 1.51 us  [the longest x1 1.33 us: body(): scalars = jnp.stack((shift, place, below, above))]
    mul x2 -> x0, local copies, waits for them, and re-layouts: 3.99 us -> none  [body(): phase = jnp.stack((jnp.cos(phase) * scale, jnp.sin(phase) * scale))]
    slice x2, local copies, waits for them, and re-layouts: 3.16 us -> 0.03 us  [body(): wide = jnp.where(part == h, value[:, h][..., None], wide)]
  transfers between devices with their start and end apart: 12 -> 12, of which waited for: 9 -> 9; matrix products, arithmetic and copies ran while one was open for 13% -> 6% of each run, Pallas kernels for 3% -> 4%
where the time goes in v2:
time: 169 us; the launch traced here: 167 us
  waiting for transfers between devices  78 us (46%)
  starting transfers between devices  51.7 us (31%)
  Pallas kernels  20.4 us (12%)
  local copies, waits for them, and re-layouts  7.79 us (5%)
  other arithmetic  6.71 us (4%)
  between operations  2.18 us (1%)
    ppermute x6, waiting for transfers between devices, body(): blocks.append(lax.ppermute(block, 'range', route))  43.4 us
    all_to_all x2, waiting for transfers between devices, body(): lax.all_to_all(blocks, ('pulse', 'range'), split_axis=0, concat_axis=0, t...  22.2 us
    all_to_all x2, starting transfers between devices, body(): lax.all_to_all(blocks, ('pulse', 'range'), split_axis=0, concat_axis=0, t...  21.4 us
    ppermute x6, starting transfers between devices, body(): blocks.append(lax.ppermute(block, 'range', route))  18.6 us
    ppermute x4, waiting for transfers between devices, shifted(): return lax.ppermute(block, 'band', route)  12.4 us
    ppermute x4, starting transfers between devices, shifted(): return lax.ppermute(block, 'band', route)  11.7 us
    pallas_call x2, Pallas kernels, range_stage(): pl.pallas_call(functools.partial(range_kernel, outer, sub, sources), grid...  8.05 us
    pallas_call x1, Pallas kernels, azimuth_stage(): pl.pallas_call(functools.partial(azimuth_kernel, outer), grid=(count // b...  7.64 us
  transfers between devices with their start and end apart: 12, of which 9 were waited for; matrix products, arithmetic and copies ran while one was open for 6% of the time, Pallas kernels for 4%

profile of v2, /device:TPU:2, one launch (start us, length us, event | category | flops | bytes accessed | tf_op | source)
XLA Modules:
  0.0 166.8 jit_solution(7205509651399024751)
XLA Ops:
  0.0 2.0 %dynamic-slice_bitcast_fusion = (bf16[2,64,1024]{2,1,0:T(8,128)(2,1)S(1)}, bf16[2,64,1024]{2,1,0:T(8,128)(2,1)}, bf16[2,64,1024]{2,1,0:T(8,128)(2,1)}) fusion(bf16[1,2,512,1024]{3,2,1,0:T(8,128)(2,1)} %param.12, s32[]{:T(128)S(6)} %select_n.175, s32[]{:T(128)S(6)} %select_n.173, s32[]{:T(128)S(6)} %select_n.171), kind=kLoop, calls=%fused_computation.3 | loop fusion | bytes 1572876 | tf_op jit(solution)/shard_map/dynamic_slice | solution.py:401
  2.0 6.3 %collective-permute-start = (bf16[2,64,1024]{2,1,0:T(8,128)(2,1)}, bf16[2,64,1024]{2,1,0:T(8,128)(2,1)S(1)}, u32[]{:S(2)}, u32[]{:S(2)}) collective-permute-start(bf16[2,64,1024]{2,1,0:T(8,128)(2,1)} %get-tuple-element.21), channel_id=1, source_target_pairs={{0,3},{1,0},{2,1},{3,2},{4,7},{5,4},{6,5},{7,6},{8,11},{9,8},{10,9... | collective-permute-start | bytes 786440 | tf_op jit(solution)/shard_map/ppermute | solution.py:403
  9.2 2.9 %collective-permute-start.2 = (bf16[2,64,1024]{2,1,0:T(8,128)(2,1)S(1)}, bf16[2,64,1024]{2,1,0:T(8,128)(2,1)S(1)}, u32[]{:S(2)}, u32[]{:S(2)}) collective-permute-start(bf16[2,64,1024]{2,1,0:T(8,128)(2,1)S(1)} %get-tuple-element.19), channel_id=1, source_target_pairs={{0,1},{1,2},{2,3},{3,0},{4,5},{5,6},{6,7},{7,4},{8,9},{9,10},{10,1... | collective-permute-start | bytes 786440 | tf_op jit(solution)/shard_map/ppermute | solution.py:403
  12.1 1.4 fusion.26
  17.5 1.2 fusion.7
  19.1 1.1 broadcast_select_fusion.1
  20.2 1.3 pad_add_fusion.scalar_ref
  21.7 9.3 %collective-permute-done.refs_0_ = bf16[2,64,1024]{2,1,0:T(8,128)(2,1)S(1)} collective-permute-done((bf16[2,64,1024]{2,1,0:T(8,128)(2,1)}, bf16[2,64,1024]{2,1,0:T(8,128)(2,1)S(1)}, u32[]{:S(2)}, u32[]{:S(2)}) %collective-permute-start) | collective-permute-done | bytes 262176 | tf_op jit(solution)/shard_map/ppermute | solution.py:403
  31.1 4.0 %range_stage.2 = (bf16[3072,128]{1,0:T(8,128)(2,1)S(1)}, bf16[1024,128]{1,0:T(8,128)(2,1)S(1)}) custom-call(s32[4]{0:T(128)S(1)} %pad_add_fusion.scalar_ref, bf16[2,4,2,64,1024]{4,3,2,1,0:T(8,128)(2,1)S(1)} %bitcast.42, bf16[2,64,1024]{2,1,0:T(8,128)(2,1)S(1)} %collective-permute-done.refs_0_, bf16[2,64,1024]{2,1,0:T(8,128)(2,1)S(1)} %collective-permute-done.1.refs_1_, ...), custom_call_target="tpu_custom_call" | custom-call | tf_op jit(solution)/shard_map/range_stage/pallas_call | solution.py:172
  35.1 3.4 %collective-permute-start.3 = (bf16[1024,128]{1,0:T(8,128)(2,1)S(1)}, bf16[1024,128]{1,0:T(8,128)(2,1)S(1)}, u32[]{:S(2)}, u32[]{:S(2)}) collective-permute-start(bf16[1024,128]{1,0:T(8,128)(2,1)S(1)} %get-tuple-element.10), channel_id=1, source_target_pairs={{0,64},{64,128},{128,192},{1,65},{65,129},{129,193},{2,66},{66,130... | collective-permute-start | bytes 786440 | tf_op jit(solution)/shard_map/ppermute | solution.py:341
  38.5 2.4 %collective-permute-start.4 = (bf16[1024,128]{1,0:T(8,128)(2,1)S(1)}, bf16[1024,128]{1,0:T(8,128)(2,1)S(1)}, u32[]{:S(2)}, u32[]{:S(2)}) collective-permute-start(bf16[1024,128]{1,0:T(8,128)(2,1)S(1)} %get-tuple-element.10), channel_id=1, source_target_pairs={{64,0},{128,64},{192,128},{65,1},{129,65},{193,129},{66,2},{130,66... | collective-permute-start | bytes 786440 | tf_op jit(solution)/shard_map/ppermute | solution.py:341
  41.0 2.4 %collective-permute-done.3.low_ref = bf16[1024,128]{1,0:T(8,128)(2,1)S(1)} collective-permute-done((bf16[1024,128]{1,0:T(8,128)(2,1)S(1)}, bf16[1024,128]{1,0:T(8,128)(2,1)S(1)}, u32[]{:S(2)}, u32[]{:S(2)}) %collective-permute-start.3) | collective-permute-done | bytes 262176 | tf_op jit(solution)/shard_map/ppermute | solution.py:341
  43.4 3.4 %collective-permute-done.4.high_ref = bf16[1024,128]{1,0:T(8,128)(2,1)S(1)} collective-permute-done((bf16[1024,128]{1,0:T(8,128)(2,1)S(1)}, bf16[1024,128]{1,0:T(8,128)(2,1)S(1)}, u32[]{:S(2)}, u32[]{:S(2)}) %collective-permute-start.4) | collective-permute-done | bytes 262176 | tf_op jit(solution)/shard_map/ppermute | solution.py:341
  46.8 2.3 %stitch.2.refs_8_ = bf16[3072,128]{1,0:T(8,128)(2,1)} custom-call(s32[4]{0:T(128)S(1)} %pad_add_fusion.scalar_ref, bf16[3072,128]{1,0:T(8,128)(2,1)S(1)} %get-tuple-element.9.own_ref, bf16[1024,128]{1,0:T(8,128)(2,1)S(1)} %collective-permute-done.3.low_ref, bf16[1024,128]{1,0:T(8,128)(2,1)S(1)} %collective-permute-done.4.high_ref), custom_call_target="tpu_custom_call" | custom-call | tf_op jit(solution)/shard_map/stitch/pallas_call | solution.py:233
  49.1 13.9 %all-to-all-start = ((bf16[64,24,2,128]{3,2,1,0:T(2,128)(2,1)}), bf16[64,24,2,128]{3,2,1,0:T(2,128)(2,1)S(1)}, u32[]{:S(2)}, u32[]{:S(2)}) async-start(bf16[64,24,2,128]{3,2,1,0:T(2,128)(2,1)} %bitcast.21), calls=%async_computation | async-start | bytes 1572864 | tf_op jit(solution)/shard_map/all_to_all | solution.py:423
  63.0 1.2 constant_dynamic-slice_fusion
  64.2 3.8 %collective-permute-start.5 = (bf16[2,64,1024]{2,1,0:T(8,128)(2,1)S(1)}, bf16[2,64,1024]{2,1,0:T(8,128)(2,1)S(1)}, u32[]{:S(2)}, u32[]{:S(2)}) collective-permute-start(bf16[2,64,1024]{2,1,0:T(8,128)(2,1)S(1)} %get-tuple-element.18), channel_id=1, source_target_pairs={{0,3},{1,0},{2,1},{3,2},{4,7},{5,4},{6,5},{7,6},{8,11},{9,8},{10,9... | collective-permute-start | bytes 786440 | tf_op jit(solution)/shard_map/ppermute | solution.py:403
  68.0 2.4 %collective-permute-start.6 = (bf16[2,64,1024]{2,1,0:T(8,128)(2,1)S(1)}, bf16[2,64,1024]{2,1,0:T(8,128)(2,1)S(1)}, u32[]{:S(2)}, u32[]{:S(2)}) collective-permute-start(bf16[2,64,1024]{2,1,0:T(8,128)(2,1)S(1)} %get-tuple-element.17), channel_id=1, source_target_pairs={{0,2},{1,3},{2,0},{3,1},{4,6},{5,7},{6,4},{7,5},{8,10},{9,11},{10,... | collective-permute-start | bytes 786440 | tf_op jit(solution)/shard_map/ppermute | solution.py:403
  70.4 2.4 %collective-permute-start.7 = (bf16[2,64,1024]{2,1,0:T(8,128)(2,1)S(1)}, bf16[2,64,1024]{2,1,0:T(8,128)(2,1)S(1)}, u32[]{:S(2)}, u32[]{:S(2)}) collective-permute-start(bf16[2,64,1024]{2,1,0:T(8,128)(2,1)S(1)} %get-tuple-element.16), channel_id=1, source_target_pairs={{0,1},{1,2},{2,3},{3,0},{4,5},{5,6},{6,7},{7,4},{8,9},{9,10},{10,1... | collective-permute-start | bytes 786440 | tf_op jit(solution)/shard_map/ppermute | solution.py:403
  72.7 23.6 %collective-permute-done.5.refs_0_ = bf16[2,64,1024]{2,1,0:T(8,128)(2,1)S(1)} collective-permute-done((bf16[2,64,1024]{2,1,0:T(8,128)(2,1)S(1)}, bf16[2,64,1024]{2,1,0:T(8,128)(2,1)S(1)}, u32[]{:S(2)}, u32[]{:S(2)}) %collective-permute-start.5) | collective-permute-done | bytes 262176 | tf_op jit(solution)/shard_map/ppermute | solution.py:403
  96.4 6.9 %collective-permute-done.6.refs_1_ = bf16[2,64,1024]{2,1,0:T(8,128)(2,1)S(1)} collective-permute-done((bf16[2,64,1024]{2,1,0:T(8,128)(2,1)S(1)}, bf16[2,64,1024]{2,1,0:T(8,128)(2,1)S(1)}, u32[]{:S(2)}, u32[]{:S(2)}) %collective-permute-start.6) | collective-permute-done | bytes 262176 | tf_op jit(solution)/shard_map/ppermute | solution.py:403
  103.3 3.5 %collective-permute-done.7.refs_2_ = bf16[2,64,1024]{2,1,0:T(8,128)(2,1)S(1)} collective-permute-done((bf16[2,64,1024]{2,1,0:T(8,128)(2,1)S(1)}, bf16[2,64,1024]{2,1,0:T(8,128)(2,1)S(1)}, u32[]{:S(2)}, u32[]{:S(2)}) %collective-permute-start.7) | collective-permute-done | bytes 262176 | tf_op jit(solution)/shard_map/ppermute | solution.py:403
  106.8 1.6 copy-done.1
  108.4 4.0 %range_stage.3 = (bf16[3072,128]{1,0:T(8,128)(2,1)S(1)}, bf16[1024,128]{1,0:T(8,128)(2,1)S(1)}) custom-call(s32[4]{0:T(128)S(1)} %pad_add_fusion.scalar_ref, bf16[2,4,2,64,1024]{4,3,2,1,0:T(8,128)(2,1)S(1)} %bitcast.43, bf16[2,64,1024]{2,1,0:T(8,128)(2,1)S(1)} %collective-permute-done.5.refs_0_, bf16[2,64,1024]{2,1,0:T(8,128)(2,1)S(1)} %collective-permute-done.6.refs_1_, ...), custom_call_target="tpu_custom_call" | custom-call | tf_op jit(solution)/shard_map/range_stage/pallas_call | solution.py:172
  112.5 3.1 %collective-permute-start.8 = (bf16[1024,128]{1,0:T(8,128)(2,1)S(1)}, bf16[1024,128]{1,0:T(8,128)(2,1)S(1)}, u32[]{:S(2)}, u32[]{:S(2)}) collective-permute-start(bf16[1024,128]{1,0:T(8,128)(2,1)S(1)} %get-tuple-element.12), channel_id=1, source_target_pairs={{0,64},{64,128},{128,192},{1,65},{65,129},{129,193},{2,66},{66,130... | collective-permute-start | bytes 786440 | tf_op jit(solution)/shard_map/ppermute | solution.py:341
  115.6 2.8 %collective-permute-start.9 = (bf16[1024,128]{1,0:T(8,128)(2,1)S(1)}, bf16[1024,128]{1,0:T(8,128)(2,1)S(1)}, u32[]{:S(2)}, u32[]{:S(2)}) collective-permute-start(bf16[1024,128]{1,0:T(8,128)(2,1)S(1)} %get-tuple-element.12), channel_id=1, source_target_pairs={{64,0},{128,64},{192,128},{65,1},{129,65},{193,129},{66,2},{130,66... | collective-permute-start | bytes 786440 | tf_op jit(solution)/shard_map/ppermute | solution.py:341
  118.3 3.8 %collective-permute-done.8.low_ref = bf16[1024,128]{1,0:T(8,128)(2,1)S(1)} collective-permute-done((bf16[1024,128]{1,0:T(8,128)(2,1)S(1)}, bf16[1024,128]{1,0:T(8,128)(2,1)S(1)}, u32[]{:S(2)}, u32[]{:S(2)}) %collective-permute-start.8) | collective-permute-done | bytes 262176 | tf_op jit(solution)/shard_map/ppermute | solution.py:341
  122.1 2.8 %collective-permute-done.9.high_ref = bf16[1024,128]{1,0:T(8,128)(2,1)S(1)} collective-permute-done((bf16[1024,128]{1,0:T(8,128)(2,1)S(1)}, bf16[1024,128]{1,0:T(8,128)(2,1)S(1)}, u32[]{:S(2)}, u32[]{:S(2)}) %collective-permute-start.9) | collective-permute-done | bytes 262176 | tf_op jit(solution)/shard_map/ppermute | solution.py:341
  124.9 2.3 %stitch.3 = bf16[3072,128]{1,0:T(8,128)(2,1)} custom-call(s32[4]{0:T(128)S(1)} %pad_add_fusion.scalar_ref, bf16[3072,128]{1,0:T(8,128)(2,1)S(1)} %get-tuple-element.11.own_ref, bf16[1024,128]{1,0:T(8,128)(2,1)S(1)} %collective-permute-done.8.low_ref, bf16[1024,128]{1,0:T(8,128)(2,1)S(1)} %collective-permute-done.9.high_ref), custom_call_target="tpu_custom_call" | custom-call | tf_op jit(solution)/shard_map/stitch/pallas_call | solution.py:233
  127.3 7.5 %all-to-all-start.1 = ((bf16[64,24,2,128]{3,2,1,0:T(2,128)(2,1)}), bf16[64,24,2,128]{3,2,1,0:T(2,128)(2,1)S(1)}, u32[]{:S(2)}, u32[]{:S(2)}) async-start(bf16[64,24,2,128]{3,2,1,0:T(2,128)(2,1)} %bitcast.26), calls=%async_computation.1 | async-start | bytes 1572864 | tf_op jit(solution)/shard_map/all_to_all | solution.py:423
  136.1 22.2 %all-to-all-done.1 = bf16[64,24,2,128]{3,2,1,0:T(2,128)(2,1)S(1)} async-done(((bf16[64,24,2,128]{3,2,1,0:T(2,128)(2,1)}), bf16[64,24,2,128]{3,2,1,0:T(2,128)(2,1)S(1)}, u32[]{:S(2)}, u32[]{:S(2)}) %all-to-all-start.1) | async-done | bytes 786464 | tf_op jit(solution)/shard_map/all_to_all | solution.py:423
  159.2 7.6 %azimuth_stage.1 = bf16[48,128,128]{2,1,0:T(8,128)(2,1)} custom-call(bf16[2,128,128]{2,1,0:T(8,128)(2,1)S(1)} %copy-done.4, bf16[2,256,256]{2,1,0:T(8,128)(2,1)S(1)} %copy-done.3, f32[2,64,128]{2,1,0:T(8,128)S(1)} %copy-done.5, f32[2,64,128]{2,1,0:T(8,128)S(1)} %pad_maximum_fusion.3.filter_ref, bf16[2,256,256]{2,1,0:T(8,128)(2,1)S(1)} %copy-done.2, ...), custom_call_target="tpu_custom_call" | custom-call | tf_op jit(solution)/shard_map/azimuth_stage/pallas_call | solution.py:324
  (54 shorter events, 5.6 us)
Async XLA Ops:
  2.0 29.1 %collective-permute-start = (bf16[2,64,1024]{2,1,0:T(8,128)(2,1)}, bf16[2,64,1024]{2,1,0:T(8,128)(2,1)S(1)}, u32[]{:S(2)}, u32[]{:S(2)}) collective-permute-start(bf16[2,64,1024]{2,1,0:T(8,128)(2,1)} %get-tuple-element.21), channel_id=1, source_target_pairs={{0,3},{1,0},{2,1},{3,2},{4,7},{5,4},{6,5},{7,6},{8,11},{9,8},{10,9... | collective-permute-start | bytes 786440 | tf_op jit(solution)/shard_map/ppermute | solution.py:403
  8.3 22.8 %collective-permute-start.1 = (bf16[2,64,1024]{2,1,0:T(8,128)(2,1)}, bf16[2,64,1024]{2,1,0:T(8,128)(2,1)S(1)}, u32[]{:S(2)}, u32[]{:S(2)}) collective-permute-start(bf16[2,64,1024]{2,1,0:T(8,128)(2,1)} %get-tuple-element.20), channel_id=1, source_target_pairs={{0,2},{1,3},{2,0},{3,1},{4,6},{5,7},{6,4},{7,5},{8,10},{9,11},{10,... | collective-permute-start | bytes 786440 | tf_op jit(solution)/shard_map/ppermute | solution.py:403
  9.2 21.9 %collective-permute-start.2 = (bf16[2,64,1024]{2,1,0:T(8,128)(2,1)S(1)}, bf16[2,64,1024]{2,1,0:T(8,128)(2,1)S(1)}, u32[]{:S(2)}, u32[]{:S(2)}) collective-permute-start(bf16[2,64,1024]{2,1,0:T(8,128)(2,1)S(1)} %get-tuple-element.19), channel_id=1, source_target_pairs={{0,1},{1,2},{2,3},{3,0},{4,5},{5,6},{6,7},{7,4},{8,9},{9,10},{10,1... | collective-permute-start | bytes 786440 | tf_op jit(solution)/shard_map/ppermute | solution.py:403
  21.6 9.5 %copy-start = (bf16[1,2,512,1024]{3,2,1,0:T(8,128)(2,1)S(1)}, bf16[1,2,512,1024]{3,2,1,0:T(8,128)(2,1)}, u32[]{:S(2)}) copy-start(bf16[1,2,512,1024]{3,2,1,0:T(8,128)(2,1)} %param.12) | copy-start | bytes 6291460
  21.6 9.5 %copy-start.2 = (bf16[2,256,256]{2,1,0:T(8,128)(2,1)S(1)}, bf16[2,256,256]{2,1,0:T(8,128)(2,1)}, u32[]{:S(2)}) copy-start(bf16[2,256,256]{2,1,0:T(8,128)(2,1)} %constant.141.clone.refs_7_.back_ref) | copy-start | bytes 786436
  35.1 8.3 %collective-permute-start.3 = (bf16[1024,128]{1,0:T(8,128)(2,1)S(1)}, bf16[1024,128]{1,0:T(8,128)(2,1)S(1)}, u32[]{:S(2)}, u32[]{:S(2)}) collective-permute-start(bf16[1024,128]{1,0:T(8,128)(2,1)S(1)} %get-tuple-element.10), channel_id=1, source_target_pairs={{0,64},{64,128},{128,192},{1,65},{65,129},{129,193},{2,66},{66,130... | collective-permute-start | bytes 786440 | tf_op jit(solution)/shard_map/ppermute | solution.py:341
  38.5 8.3 %collective-permute-start.4 = (bf16[1024,128]{1,0:T(8,128)(2,1)S(1)}, bf16[1024,128]{1,0:T(8,128)(2,1)S(1)}, u32[]{:S(2)}, u32[]{:S(2)}) collective-permute-start(bf16[1024,128]{1,0:T(8,128)(2,1)S(1)} %get-tuple-element.10), channel_id=1, source_target_pairs={{64,0},{128,64},{192,128},{65,1},{129,65},{193,129},{66,2},{130,66... | collective-permute-start | bytes 786440 | tf_op jit(solution)/shard_map/ppermute | solution.py:341
  49.1 23.6 %copy-start.7 = (f32[1,128,128]{2,1,0:T(8,128)S(1)}, f32[1,128,128]{2,1,0:T(8,128)}, u32[]{:S(2)}) copy-start(f32[1,128,128]{2,1,0:T(8,128)} %get-tuple-element.35) | copy-start | bytes 196612
  49.1 78.2 %all-to-all-start = ((bf16[64,24,2,128]{3,2,1,0:T(2,128)(2,1)}), bf16[64,24,2,128]{3,2,1,0:T(2,128)(2,1)S(1)}, u32[]{:S(2)}, u32[]{:S(2)}) async-start(bf16[64,24,2,128]{3,2,1,0:T(2,128)(2,1)} %bitcast.21), calls=%async_computation | async-start | bytes 1572864 | tf_op jit(solution)/shard_map/all_to_all | solution.py:423
  64.2 32.1 %collective-permute-start.5 = (bf16[2,64,1024]{2,1,0:T(8,128)(2,1)S(1)}, bf16[2,64,1024]{2,1,0:T(8,128)(2,1)S(1)}, u32[]{:S(2)}, u32[]{:S(2)}) collective-permute-start(bf16[2,64,1024]{2,1,0:T(8,128)(2,1)S(1)} %get-tuple-element.18), channel_id=1, source_target_pairs={{0,3},{1,0},{2,1},{3,2},{4,7},{5,4},{6,5},{7,6},{8,11},{9,8},{10,9... | collective-permute-start | bytes 786440 | tf_op jit(solution)/shard_map/ppermute | solution.py:403
  68.0 35.3 %collective-permute-start.6 = (bf16[2,64,1024]{2,1,0:T(8,128)(2,1)S(1)}, bf16[2,64,1024]{2,1,0:T(8,128)(2,1)S(1)}, u32[]{:S(2)}, u32[]{:S(2)}) collective-permute-start(bf16[2,64,1024]{2,1,0:T(8,128)(2,1)S(1)} %get-tuple-element.17), channel_id=1, source_target_pairs={{0,2},{1,3},{2,0},{3,1},{4,6},{5,7},{6,4},{7,5},{8,10},{9,11},{10,... | collective-permute-start | bytes 786440 | tf_op jit(solution)/shard_map/ppermute | solution.py:403
  70.4 36.5 %collective-permute-start.7 = (bf16[2,64,1024]{2,1,0:T(8,128)(2,1)S(1)}, bf16[2,64,1024]{2,1,0:T(8,128)(2,1)S(1)}, u32[]{:S(2)}, u32[]{:S(2)}) collective-permute-start(bf16[2,64,1024]{2,1,0:T(8,128)(2,1)S(1)} %get-tuple-element.16), channel_id=1, source_target_pairs={{0,1},{1,2},{2,3},{3,0},{4,5},{5,6},{6,7},{7,4},{8,9},{9,10},{10,1... | collective-permute-start | bytes 786440 | tf_op jit(solution)/shard_map/ppermute | solution.py:403
  106.8 1.6 copy-start.1
  112.4 22.4 %copy-start.8 = (f32[8192]{0:T(1024)S(1)}, f32[8192]{0:T(1024)}, u32[]{:S(2)}) copy-start(f32[8192]{0:T(1024)} %param.16) | copy-start | bytes 98308
  112.5 9.6 %collective-permute-start.8 = (bf16[1024,128]{1,0:T(8,128)(2,1)S(1)}, bf16[1024,128]{1,0:T(8,128)(2,1)S(1)}, u32[]{:S(2)}, u32[]{:S(2)}) collective-permute-start(bf16[1024,128]{1,0:T(8,128)(2,1)S(1)} %get-tuple-element.12), channel_id=1, source_target_pairs={{0,64},{64,128},{128,192},{1,65},{65,129},{129,193},{2,66},{66,130... | collective-permute-start | bytes 786440 | tf_op jit(solution)/shard_map/ppermute | solution.py:341
  115.6 9.4 %collective-permute-start.9 = (bf16[1024,128]{1,0:T(8,128)(2,1)S(1)}, bf16[1024,128]{1,0:T(8,128)(2,1)S(1)}, u32[]{:S(2)}, u32[]{:S(2)}) collective-permute-start(bf16[1024,128]{1,0:T(8,128)(2,1)S(1)} %get-tuple-element.12), channel_id=1, source_target_pairs={{64,0},{128,64},{192,128},{65,1},{129,65},{193,129},{66,2},{130,66... | collective-permute-start | bytes 786440 | tf_op jit(solution)/shard_map/ppermute | solution.py:341
  127.3 31.1 %all-to-all-start.1 = ((bf16[64,24,2,128]{3,2,1,0:T(2,128)(2,1)}), bf16[64,24,2,128]{3,2,1,0:T(2,128)(2,1)S(1)}, u32[]{:S(2)}, u32[]{:S(2)}) async-start(bf16[64,24,2,128]{3,2,1,0:T(2,128)(2,1)} %bitcast.26), calls=%async_computation.1 | async-start | bytes 1572864 | tf_op jit(solution)/shard_map/all_to_all | solution.py:423
  134.8 24.3 %copy-start.3 = (bf16[2,256,256]{2,1,0:T(8,128)(2,1)S(1)}, bf16[2,256,256]{2,1,0:T(8,128)(2,1)}, u32[]{:S(2)}) copy-start(bf16[2,256,256]{2,1,0:T(8,128)(2,1)} %constant.143.clone.fore_ref) | copy-start | bytes 786436
  134.9 24.3 %copy-start.4 = (bf16[2,128,128]{2,1,0:T(8,128)(2,1)S(1)}, bf16[2,128,128]{2,1,0:T(8,128)(2,1)}, u32[]{:S(2)}) copy-start(bf16[2,128,128]{2,1,0:T(8,128)(2,1)} %constant.142.clone.first_ref) | copy-start | bytes 196612
  134.9 24.3 %copy-start.5 = (f32[2,64,128]{2,1,0:T(8,128)S(1)}, f32[2,64,128]{2,1,0:T(8,128)}, u32[]{:S(2)}) copy-start(f32[2,64,128]{2,1,0:T(8,128)} %constant.144.clone.twist_ref) | copy-start | bytes 196612
  134.9 24.3 %copy-start.6 = (bf16[2,128,128]{2,1,0:T(8,128)(2,1)S(1)}, bf16[2,128,128]{2,1,0:T(8,128)(2,1)}, u32[]{:S(2)}) copy-start(bf16[2,128,128]{2,1,0:T(8,128)(2,1)} %constant.145.clone.last_ref) | copy-start | bytes 196612
